TPU v7x, 128 devices: a whole 4x4x4 slice. The times are simulated.
128 devices in a mesh: expert: 4 (over z), shard: 32 (over y, x, core).
Axes of the slice: x: 4, y: 4, z: 4, core: 2. Of those that a mesh axis runs over, the one named last changes fastest.
Arguments:
- master_gate: float32 [64, 2048, 1408], P('expert', 'shard'), may hold values from -0.25 to 0.25
- master_up: float32 [64, 2048, 1408], P('expert', 'shard'), may hold values from -0.25 to 0.25
- router_weight: float32 [2048, 64], P('shard', 'expert'), may hold values from -0.125 to 0.125
- router_gain: float32 [2048], P('shard'), may hold values from 0.25 to 1.75
Outputs:
- final_gate: bfloat16 [64, 2048, 1408], P('expert', None, 'shard')
- final_up: bfloat16 [64, 2048, 1408], P('expert', None, 'shard')
- scale_gate: float32 [64, 1408], P('expert', 'shard')
- scale_up: float32 [64, 1408], P('expert', 'shard')
- serve_router: bfloat16 [2048, 64], replicated
All inputs are finite; a program needn't handle non-finite values.
Results may differ from a plain program's by a relative error of at most 0.001.
Values may be sent and summed in bfloat16 or wider, within the bound.
A program may use at most 128 MiB of HBM per device.

v0:
```python
import jax
import jax.numpy as jnp
from jax import lax
from jax.sharding import PartitionSpec as P


def sent_to_all(array, axis):
    copies = jnp.broadcast_to(array, (lax.axis_size(axis), *array.shape))
    return lax.all_to_all(copies, axis, split_axis=0, concat_axis=0, tiled=True)


def over_copies(array, axis):
    everything = sent_to_all(array, axis)
    return jnp.sum(everything, axis=0)


def packed_total(arrays, axis):
    ends = [0]
    for a in arrays:
        ends.append(ends[-1] + a.size)
    total = over_copies(jnp.concatenate([a.ravel() for a in arrays]), axis)
    return tuple((total[b:e].reshape(a.shape) for a, b, e in zip(arrays, ends, ends[1:])))


def joined_along(parts, dim):
    parts = jnp.moveaxis(parts, 0, dim)
    shape = parts.shape
    return parts.reshape(*shape[:dim], shape[dim] * shape[dim + 1], *shape[dim + 2 :])


def gathered_copies(array, axis, dim):
    parts = sent_to_all(array, axis)
    return joined_along(parts, dim)


def local(master_gate, master_up, router_weight, router_gain):
    total_gate, total_up = packed_total(
        (jnp.sum(master_gate * master_gate, axis=1), jnp.sum(master_up * master_up, axis=1)),
        "shard",
    )
    scale_gate = jnp.sqrt(total_gate)
    scale_up = jnp.sqrt(total_up)
    narrow_gate, narrow_up = (
        (master_gate / jnp.expand_dims(scale_gate, 1)).astype(jnp.bfloat16),
        (master_up / jnp.expand_dims(scale_up, 1)).astype(jnp.bfloat16),
    )
    final_gate, final_up = (
        lax.all_to_all(narrow_gate, "shard", split_axis=2, concat_axis=1, tiled=True),
        lax.all_to_all(narrow_up, "shard", split_axis=2, concat_axis=1, tiled=True),
    )
    scale_gate = lax.dynamic_slice_in_dim(
        scale_gate, lax.axis_index("shard") * final_gate.shape[2], final_gate.shape[2], axis=1
    )
    scale_up = lax.dynamic_slice_in_dim(
        scale_up, lax.axis_index("shard") * final_up.shape[2], final_up.shape[2], axis=1
    )
    part_router = (router_weight * router_gain[:, None]).astype(jnp.bfloat16)
    row_router = gathered_copies(part_router, "shard", 0)
    serve_router = gathered_copies(row_router, "expert", 1)
    return (final_gate, final_up, scale_gate, scale_up, serve_router)


def solution(mesh):
    in_specs = (
        P("expert", "shard", None),
        P("expert", "shard", None),
        P("shard", "expert"),
        P("shard"),
    )
    out_specs = (
        P("expert", None, "shard"),
        P("expert", None, "shard"),
        P("expert", "shard"),
        P("expert", "shard"),
        P(),
    )
    return jax.shard_map(local, mesh=mesh, in_specs=in_specs, out_specs=out_specs, check_vma=False)
```

profile of v0, /device:TPU:1, one launch (start us, length us, event | category | flops | bytes accessed | tf_op | source)
XLA Modules:
  0.0 249.9 jit_solution(871266598560008006)
XLA Ops:
  0.6 0.7 multiply_convert_fusion
  1.4 0.8 reshape.57
  2.1 8.6 %all-to-all-start.3 = ((bf16[32,2,512]{2,1,0:T(2,128)(2,1)}), bf16[32,2,512]{2,1,0:T(2,128)(2,1)S(1)}, u32[]{:S(2)}, u32[]{:S(2)}) async-start(bf16[32,2,512]{2,1,0:T(2,128)(2,1)} %reshape.57), calls=%async_computation.3 | async-start | bytes 131072 | tf_op jit(solution)/shard_map/all_to_all | solution.py:9
  10.7 3.2 %multiply_reduce_fusion.1 = f32[16,1408]{1,0:T(8,128)S(1)} fusion(f32[16,64,1408]{2,1,0:T(8,128)} %param.4), kind=kLoop, calls=%fused_computation.3 | loop fusion | flops 2861056 | bytes 5857280 | tf_op jit(solution)/shard_map/reduce_sum | solution.py:38
  14.0 3.2 %multiply_reduce_fusion = f32[16,1408]{1,0:T(8,128)S(1)} fusion(f32[16,64,1408]{2,1,0:T(8,128)} %param.5), kind=kLoop, calls=%fused_computation.2 | loop fusion | flops 2861056 | bytes 5857280 | tf_op jit(solution)/shard_map/reduce_sum | solution.py:38
  17.2 0.8 all-to-all-done.3
  18.0 7.7 %broadcast_in_dim.12 = f32[32,1,45056]{2,1,0:T(1,128)} broadcast(f32[45056]{0:T(1024)S(1)} %pad_maximum_fusion), dimensions={2} | broadcast | bytes 5947392 | tf_op jit(solution)/shard_map/broadcast_in_dim | solution.py:8
  25.7 6.6 %all-to-all-start = ((f32[32,1,45056]{2,1,0:T(1,128)}), f32[32,1,45056]{2,1,0:T(1,128)}, u32[]{:S(2)}, u32[]{:S(2)}) async-start(f32[32,1,45056]{2,1,0:T(1,128)} %broadcast_in_dim.12), calls=%async_computation | async-start | bytes 11534336 | tf_op jit(solution)/shard_map/all_to_all | solution.py:9
  32.3 10.8 %copy.43 = f32[16,64,1408]{1,0,2:T(8,128)} copy(f32[16,64,1408]{2,1,0:T(8,128)} %param.4) | data formatting | bytes 11534336 | tf_op args[0]
  43.5 56.4 %all-to-all-done = f32[32,1,45056]{2,1,0:T(1,128)} async-done(((f32[32,1,45056]{2,1,0:T(1,128)}), f32[32,1,45056]{2,1,0:T(1,128)}, u32[]{:S(2)}, u32[]{:S(2)}) %all-to-all-start) | async-done | bytes 5767200 | tf_op jit(solution)/shard_map/all_to_all | solution.py:9
  99.9 0.7 broadcast_in_dim.14
  100.7 5.0 %all-to-all-start.4 = ((bf16[4,2048,16]{1,2,0:T(8,128)(2,1)}), bf16[4,2048,16]{1,2,0:T(8,128)(2,1)S(1)}, u32[]{:S(2)}, u32[]{:S(2)}) async-start(bf16[4,2048,16]{1,2,0:T(8,128)(2,1)} %broadcast_in_dim.14), calls=%async_computation.4 | async-start | bytes 524288 | tf_op jit(solution)/shard_map/all_to_all | solution.py:9
  105.7 6.4 %reduce_sum.29 = f32[45056]{0:T(1024)S(1)} reduce(f32[32,1,45056]{2,1,0:T(1,128)} %all-to-all-done, f32[]{:T(128)} %constant.5.clone.1), dimensions={0,1}, to_apply=%region_2.0 | reduce | flops 1396736 | bytes 5947396 | tf_op jit(solution)/shard_map/reduce_sum | solution.py:14
  112.1 0.3 copy.42
  112.4 10.1 %fusion = bf16[1408,16,64]{2,1,0:T(8,128)(2,1)} fusion(f32[16,64,1408]{1,0,2:T(8,128)} %copy.43, f32[16,1408]{0,1:T(8,128)S(1)} %copy.42), kind=kLoop, calls=%fused_computation.10 | loop fusion | flops 2883584 | bytes 8740864
  122.5 8.4 %reshape.53 = bf16[32,2,22528]{2,1,0:T(2,128)(2,1)} reshape(bf16[1408,16,64]{2,1,0:T(8,128)(2,1)} %fusion) | data formatting | bytes 5767168
  130.9 8.5 %all-to-all-start.1 = ((bf16[32,2,22528]{2,1,0:T(2,128)(2,1)}), bf16[32,2,22528]{2,1,0:T(2,128)(2,1)S(1)}, u32[]{:S(2)}, u32[]{:S(2)}) async-start(bf16[32,2,22528]{2,1,0:T(2,128)(2,1)} %reshape.53), calls=%async_computation.1 | async-start | bytes 5767168 | tf_op jit(solution)/shard_map/all_to_all | solution.py:48
  139.5 10.8 %copy.46 = f32[16,64,1408]{1,0,2:T(8,128)} copy(f32[16,64,1408]{2,1,0:T(8,128)} %param.5) | data formatting | bytes 11534336 | tf_op args[1]
  150.3 1.1 copy.45
  151.5 10.4 %fusion.1 = bf16[1408,16,64]{2,1,0:T(8,128)(2,1)} fusion(f32[16,64,1408]{1,0,2:T(8,128)} %copy.46, f32[16,1408]{0,1:T(8,128)} %copy.45), kind=kLoop, calls=%fused_computation.11 | loop fusion | flops 2883584 | bytes 8740864
  161.8 8.4 %reshape.55 = bf16[32,2,22528]{2,1,0:T(2,128)(2,1)} reshape(bf16[1408,16,64]{2,1,0:T(8,128)(2,1)} %fusion.1) | data formatting | bytes 5767168
  170.3 6.0 %all-to-all-done.1 = bf16[32,2,22528]{2,1,0:T(2,128)(2,1)S(1)} async-done(((bf16[32,2,22528]{2,1,0:T(2,128)(2,1)}), bf16[32,2,22528]{2,1,0:T(2,128)(2,1)S(1)}, u32[]{:S(2)}, u32[]{:S(2)}) %all-to-all-start.1) | async-done | bytes 2883616 | tf_op jit(solution)/shard_map/all_to_all | solution.py:48
  176.3 7.1 %all-to-all-start.2 = ((bf16[32,2,22528]{2,1,0:T(2,128)(2,1)}), bf16[32,2,22528]{2,1,0:T(2,128)(2,1)}, u32[]{:S(2)}, u32[]{:S(2)}) async-start(bf16[32,2,22528]{2,1,0:T(2,128)(2,1)} %reshape.55), calls=%async_computation.2 | async-start | bytes 5767168 | tf_op jit(solution)/shard_map/all_to_all | solution.py:49
  183.4 0.7 constant_dynamic-slice_fusion
  184.1 5.9 %reshape.54 = bf16[1408,16,64]{2,1,0:T(8,128)(2,1)} reshape(bf16[32,2,22528]{2,1,0:T(2,128)(2,1)S(1)} %all-to-all-done.1) | data formatting | bytes 5767168
  190.0 11.9 %copy.44 = bf16[16,32,64,44]{2,1,0,3:T(8,128)(2,1)} copy(bf16[16,32,64,44]{2,0,3,1:T(8,128)(2,1)} %bitcast.28) | data formatting | bytes 5767168 | tf_op jit(solution)/shard_map/all_to_all | solution.py:48
  201.9 8.7 %all_to_all.40 = bf16[16,2048,44]{1,0,2:T(8,128)(2,1)} reshape(bf16[16,32,64,44]{2,1,0,3:T(8,128)(2,1)} %copy.44) | data formatting | bytes 5767168 | tf_op jit(solution)/shard_map/all_to_all | solution.py:48
  210.6 9.6 %all-to-all-done.2 = bf16[32,2,22528]{2,1,0:T(2,128)(2,1)} async-done(((bf16[32,2,22528]{2,1,0:T(2,128)(2,1)}), bf16[32,2,22528]{2,1,0:T(2,128)(2,1)}, u32[]{:S(2)}, u32[]{:S(2)}) %all-to-all-start.2) | async-done | bytes 2883616 | tf_op jit(solution)/shard_map/all_to_all | solution.py:49
  220.2 8.4 %reshape.56 = bf16[1408,16,64]{2,1,0:T(8,128)(2,1)} reshape(bf16[32,2,22528]{2,1,0:T(2,128)(2,1)} %all-to-all-done.2) | data formatting | bytes 5767168
  228.6 11.9 %copy.47 = bf16[16,32,64,44]{2,1,0,3:T(8,128)(2,1)} copy(bf16[16,32,64,44]{2,0,3,1:T(8,128)(2,1)} %bitcast.29) | data formatting | bytes 5767168 | tf_op jit(solution)/shard_map/all_to_all | solution.py:49
  240.4 8.7 %all_to_all.44 = bf16[16,2048,44]{1,0,2:T(8,128)(2,1)} reshape(bf16[16,32,64,44]{2,1,0,3:T(8,128)(2,1)} %copy.47) | data formatting | bytes 5767168 | tf_op jit(solution)/shard_map/all_to_all | solution.py:49
  249.2 0.7 copy.53
  (11 shorter events, 0.5 us)
Async XLA Ops:
  2.1 15.9 %all-to-all-start.3 = ((bf16[32,2,512]{2,1,0:T(2,128)(2,1)}), bf16[32,2,512]{2,1,0:T(2,128)(2,1)S(1)}, u32[]{:S(2)}, u32[]{:S(2)}) async-start(bf16[32,2,512]{2,1,0:T(2,128)(2,1)} %reshape.57), calls=%async_computation.3 | async-start | bytes 131072 | tf_op jit(solution)/shard_map/all_to_all | solution.py:9
  25.7 74.2 %all-to-all-start = ((f32[32,1,45056]{2,1,0:T(1,128)}), f32[32,1,45056]{2,1,0:T(1,128)}, u32[]{:S(2)}, u32[]{:S(2)}) async-start(f32[32,1,45056]{2,1,0:T(1,128)} %broadcast_in_dim.12), calls=%async_computation | async-start | bytes 11534336 | tf_op jit(solution)/shard_map/all_to_all | solution.py:9
  100.7 30.3 %all-to-all-start.4 = ((bf16[4,2048,16]{1,2,0:T(8,128)(2,1)}), bf16[4,2048,16]{1,2,0:T(8,128)(2,1)S(1)}, u32[]{:S(2)}, u32[]{:S(2)}) async-start(bf16[4,2048,16]{1,2,0:T(8,128)(2,1)} %broadcast_in_dim.14), calls=%async_computation.4 | async-start | bytes 524288 | tf_op jit(solution)/shard_map/all_to_all | solution.py:9
  130.9 45.3 %all-to-all-start.1 = ((bf16[32,2,22528]{2,1,0:T(2,128)(2,1)}), bf16[32,2,22528]{2,1,0:T(2,128)(2,1)S(1)}, u32[]{:S(2)}, u32[]{:S(2)}) async-start(bf16[32,2,22528]{2,1,0:T(2,128)(2,1)} %reshape.53), calls=%async_computation.1 | async-start | bytes 5767168 | tf_op jit(solution)/shard_map/all_to_all | solution.py:48
  176.3 43.9 %all-to-all-start.2 = ((bf16[32,2,22528]{2,1,0:T(2,128)(2,1)}), bf16[32,2,22528]{2,1,0:T(2,128)(2,1)}, u32[]{:S(2)}, u32[]{:S(2)}) async-start(bf16[32,2,22528]{2,1,0:T(2,128)(2,1)} %reshape.55), calls=%async_computation.2 | async-start | bytes 5767168 | tf_op jit(solution)/shard_map/all_to_all | solution.py:49
where the time goes:
time: 253 us; the launch traced here: 250 us
  local copies, waits for them, and re-layouts  106 us (42%)
  waiting for transfers between devices  72.8 us (29%)
  starting transfers between devices  35.9 us (14%)
  other arithmetic  34 us (13%)
    all_to_all x3, waiting for transfers between devices, sent_to_all(): return lax.all_to_all(copies, axis, split_axis=0, concat_axis=0, tiled=True)  57.2 us
    unnamed x10, local copies, waits for them, and re-layouts  54.5 us
    all_to_all x2, local copies, waits for them, and re-layouts, local(): lax.all_to_all(narrow_up, 'shard', split_axis=2, concat_axis=1, tiled=True)  20.6 us
    all_to_all x2, local copies, waits for them, and re-layouts, local(): lax.all_to_all(narrow_gate, 'shard', split_axis=2, concat_axis=1, tiled=T...  20.6 us
    unnamed x2, other arithmetic  20.4 us
    all_to_all x3, starting transfers between devices, sent_to_all(): return lax.all_to_all(copies, axis, split_axis=0, concat_axis=0, tiled=True)  20.2 us
    all_to_all x1, waiting for transfers between devices, local(): lax.all_to_all(narrow_up, 'shard', split_axis=2, concat_axis=1, tiled=True)  9.59 us
    all_to_all x1, starting transfers between devices, local(): lax.all_to_all(narrow_gate, 'shard', split_axis=2, concat_axis=1, tiled=T...  8.54 us
  transfers between devices with their start and end apart: 5, of which 4 were waited for; matrix products, arithmetic and copies ran while one was open for 37% of the time, Pallas kernels for 0%

commit v1 on v0

v1 whole, which is shorter than its diff:
```python
import jax
import jax.numpy as jnp
from jax import lax
from jax.experimental import pallas as pl
from jax.experimental.pallas import tpu as pltpu
from jax.sharding import PartitionSpec as P

MESH = pl.DeviceIdType.MESH
LANES = 128
SPAN = 250.0
FLOOR = 124.0
MIX, START = 11, 16


def encoded(x, partial):
    rate = jnp.where(partial > 0, SPAN * lax.rsqrt(partial), 0.0)
    code = jnp.exp2(jnp.abs(x) * rate - FLOOR)
    return jnp.where(x < 0, -code, code)


def make_kernel(experts, rows, width, group, cols, n_y, n_x, n_z):
    n = n_y * n_x * 2
    half = experts // 2
    blocks = width // LANES
    pieces = 2
    part = cols // pieces
    prow = part * half
    n_msg = 2 * (pieces + 1)

    def kernel(gate, up, router, gain, og, ou, osg, osu, orr,
               xg, xu, stage, code, got, sums, msg, inbox, factor, zbuf, zgot,
               in_sem, own_sem, send_sem, recv_sem, zsend, zrecv):
        me = lax.axis_index("shard")
        plane = lax.axis_index("expert")
        my_y, my_x, my_k = me // (2 * n_x), (me // 2) % n_x, me % 2

        def load(h, t):
            src, dst = ((gate, xg), (up, xu))[t]
            return pltpu.make_async_copy(
                src.at[pl.ds(h * half, half)], dst.at[pl.ds(h * half, half)], in_sem.at[h, t]
            )

        for h in range(2):
            for t in range(2):
                load(h, t).start()

        def greet(d, _):
            pl.semaphore_signal(
                barrier, 1, device_id={"shard": lax.rem(me + d, n)}, device_id_type=MESH
            )
            return _

        barrier = pltpu.get_barrier_semaphore()
        lax.fori_loop(1, n, greet, 0)
        for d in range(1, n_z):
            pl.semaphore_signal(
                barrier, 1, device_id={"expert": lax.rem(plane + d, n_z)}, device_id_type=MESH
            )

        lane = lax.broadcasted_iota(jnp.int32, (half, LANES), 1)
        left = lane < LANES // 2
        folded = router[...] * gain[...]
        folded = jnp.concatenate([folded[:half], folded[half:]], axis=1)

        def produce(h):
            def block(b, _):
                at = pl.ds(pl.multiple_of(b * LANES, LANES), LANES)
                for e in range(half):
                    g = xg[h * half + e, :, at]
                    u = xu[h * half + e, :, at]
                    pg = jnp.sum(g * g, axis=0, keepdims=True)
                    pu = jnp.sum(u * u, axis=0, keepdims=True)
                    sums[h, 0, pl.ds(e, 1), at] = pg
                    sums[h, 1, pl.ds(e, 1), at] = pu
                    both = jnp.concatenate([encoded(g, pg), encoded(u, pu)], axis=0)
                    stage[pl.ds(e, LANES, stride=half), :] = both.T
                code[h, pl.ds(pl.multiple_of(b * LANES * half, LANES * half), LANES * half), :] = stage[...].astype(jnp.bfloat16)
                return _

            lax.fori_loop(0, blocks, block, 0)

            def message(q, _):
                first = q * cols
                lo = pl.multiple_of(first // LANES * LANES, LANES)
                s = lax.rem(first, LANES)
                quads = []
                for t, shift in ((0, lax.rem(LANES - s, LANES)), (1, lax.rem(LANES + LANES // 2 - s, LANES))):
                    a = sums[h, t, :, pl.ds(lo, LANES)]
                    b = sums[h, t, :, pl.ds(lo + LANES, LANES)]
                    a, b = pltpu.roll(a, shift, axis=1), pltpu.roll(b, shift, axis=1)
                    quads.append(jnp.where(lane - t * (LANES // 2) + s < LANES, a, b))
                msg[q, pl.ds(2 * h * half, half), :] = jnp.where(left, quads[0], quads[1])
                if h == 0:
                    msg[q, pl.ds(half, half), :] = folded
                return _

            lax.fori_loop(0, n, message, 0)

        def peer(d):
            y = lax.rem(my_y + d // (2 * n_x), n_y)
            x = lax.rem(my_x + (d // 2) % n_x, n_x)
            k = lax.rem(my_k + d % 2, 2)
            return (y * n_x + x) * 2 + k

        def slices(m):
            h, c = m // (pieces + 1), m % (pieces + 1)
            return h, c

        def remote(m, q, s):
            h, c = slices(m)
            if c == 0:
                rng = pl.ds(0, 2 * half) if h == 0 else pl.ds(2 * half, half)
                src, dst = msg.at[q, rng], inbox.at[s, rng]
            else:
                src = code.at[h, pl.ds(pl.multiple_of(q * cols * half + (c - 1) * prow, 2 * half), prow)]
                dst = got.at[h, s, pl.ds((c - 1) * prow, prow)]
            return pltpu.make_async_remote_copy(
                src, dst, send_sem.at[m, q], recv_sem.at[m, s],
                device_id={"shard": q}, device_id_type=MESH,
            )

        def each_peer(act):
            def one(i, _):
                act(peer(lax.rem(i * MIX + START, n)))
                return _

            skip = (-START * pow(MIX, -1, n)) % n
            lax.fori_loop(0, skip, one, 0)
            lax.fori_loop(skip + 1, n, one, 0)

        def own(h):
            return pltpu.make_async_copy(
                code.at[h, pl.ds(pl.multiple_of(me * cols * half, 2 * half), cols * half)],
                got.at[h, me], own_sem.at[h],
            )

        for h in range(2):
            for t in range(2):
                load(h, t).wait()
            produce(h)
            if h == 0:
                pl.semaphore_wait(barrier, n - 1 + n_z - 1)
            for c in range(pieces + 1):
                each_peer(lambda q: remote(h * (pieces + 1) + c, q, me).start())
            own(h).start()
            inbox[me, pl.ds(2 * h * half, half), :] = msg[me, pl.ds(2 * h * half, half), :]
            if h == 0:
                inbox[me, pl.ds(half, half), :] = folded

        def arrived(m):
            each_peer(lambda q: remote(m, me, q).wait_recv())

        arrived(0)

        def join(c, _):
            a, b = inbox[2 * c, pl.ds(half, half), :], inbox[2 * c + 1, pl.ds(half, half), :]
            low = jnp.where(left, a, pltpu.roll(b, LANES // 2, axis=1))
            high = jnp.where(left, pltpu.roll(a, LANES // 2, axis=1), b)
            zbuf[:, pl.ds(pl.multiple_of(c * LANES, LANES), LANES)] = jnp.concatenate([low, high], axis=0).astype(jnp.bfloat16)
            return _

        lax.fori_loop(0, n // 2, join, 0)

        def across(d):
            z = lax.rem(plane + d, n_z)
            return pltpu.make_async_remote_copy(
                zbuf, zgot.at[plane], zsend.at[d], zrecv.at[plane],
                device_id={"expert": z}, device_id_type=MESH,
            )

        def from_across(d):
            z = lax.rem(plane + d, n_z)
            return pltpu.make_async_remote_copy(
                zbuf, zgot.at[z], zsend.at[d], zrecv.at[z],
                device_id={"expert": z}, device_id_type=MESH,
            )

        for d in range(1, n_z):
            across(d).start()
        orr[pl.ds(pl.multiple_of(plane * experts, experts), experts), :] = zbuf[...]

        def factors(h):
            rng = pl.ds(2 * h * half, half)
            total = lax.fori_loop(0, n, lambda s, t: t + inbox[s, rng, :], jnp.zeros((half, LANES), jnp.float32))
            scale = jnp.sqrt(total)
            osg[pl.ds(h * half, half), :] = scale[:, :cols]
            osu[pl.ds(h * half, half), :] = pltpu.roll(scale, LANES // 2, axis=1)[:, :cols]
            share = 1.0 / (SPAN * scale)

            def one(s, _):
                factor[s] = jnp.sqrt(inbox[s, rng, :]) * share
                return _

            lax.fori_loop(0, n, one, 0)

        pick = jnp.where(left, 0, LANES // 2)

        def decode(h, c):
            m = h * (pieces + 1) + 1 + c

            def chip(i, _):
                dc = lax.rem(START // 2 + MIX * i, n // 2)
                y = lax.rem(my_y - dc // n_x + n_y, n_y)
                x = lax.rem(my_x - dc % n_x + n_x, n_x)
                at = y * n_x + x
                for k in range(2):
                    s = 2 * at + k

                    @pl.when(s != me)
                    def arrival():
                        remote(m, me, s).wait_recv()

                fa, fb = factor[2 * at], factor[2 * at + 1]
                lanes_out = pl.ds(pl.multiple_of(at * LANES, LANES), LANES)
                for p in range(part // 2):
                    base = c * prow + p * 2 * half
                    pair = []
                    for s, f in ((2 * at, fa), (2 * at + 1, fb)):
                        v = got[h, s, pl.ds(base, 2 * half), :].astype(jnp.float32)
                        j = c * part + 2 * p
                        mul = jnp.concatenate(
                            [jnp.take_along_axis(f, pick + j, axis=1), jnp.take_along_axis(f, pick + (j + 1), axis=1)], axis=0
                        )
                        w = (jnp.log2(jnp.abs(v)) + FLOOR) * mul
                        pair.append(jnp.where(v < 0, -w, w))
                    a, b = pair
                    l2 = jnp.concatenate([left, left], axis=0)
                    turned = pltpu.roll(jnp.where(l2, b, a), LANES // 2, axis=1)
                    fg = jnp.where(l2, a, turned).astype(jnp.bfloat16)
                    fu = jnp.where(l2, turned, b).astype(jnp.bfloat16)
                    for r in range(2):
                        og[j + r, pl.ds(h * half, half), lanes_out] = fg[r * half:(r + 1) * half]
                        ou[j + r, pl.ds(h * half, half), lanes_out] = fu[r * half:(r + 1) * half]
                return _

            lax.fori_loop(0, n // 2, chip, 0)

        for h in range(2):
            if h == 1:
                arrived(pieces + 1)
            factors(h)
            own(h).wait()
            for c in range(pieces):
                decode(h, c)

        for d in range(1, n_z):
            across(d).wait_send()
            from_across(d).wait_recv()
            z = lax.rem(plane + d, n_z)
            orr[pl.ds(pl.multiple_of(z * experts, experts), experts), :] = zgot[z]
        for m in range(n_msg):
            each_peer(lambda q: remote(m, q, me).wait_send())

    return kernel


def solution(mesh):
    n_z, n = mesh.shape["expert"], mesh.shape["shard"]
    n_y = n_x = 4

    def local(master_gate, master_up, router_weight, router_gain):
        experts, rows, width = master_gate.shape
        cols = width // n
        depth = rows * n
        half = experts // 2
        f32, bf16 = jnp.float32, jnp.bfloat16
        vmem = pl.BlockSpec(memory_space=pltpu.VMEM)
        hbm = pl.BlockSpec(memory_space=pl.ANY)
        dma = pltpu.SemaphoreType.DMA
        og, ou, osg, osu, orr = pl.pallas_call(
            make_kernel(experts, rows, width, None, cols, n_y, n_x, n_z),
            out_shape=(
                jax.ShapeDtypeStruct((cols, experts, depth), bf16),
                jax.ShapeDtypeStruct((cols, experts, depth), bf16),
                jax.ShapeDtypeStruct((experts, cols), f32),
                jax.ShapeDtypeStruct((experts, cols), f32),
                jax.ShapeDtypeStruct((experts * n_z, depth), bf16),
            ),
            in_specs=[hbm, hbm, vmem, vmem],
            out_specs=(vmem,) * 5,
            scratch_shapes=[
                pltpu.VMEM((experts, rows, width), f32),
                pltpu.VMEM((experts, rows, width), f32),
                pltpu.VMEM((LANES * half, LANES), f32),
                pltpu.VMEM((2, width * half, LANES), bf16),
                pltpu.VMEM((2, n, cols * half, LANES), bf16),
                pltpu.VMEM((2, 2, half, width + LANES), f32),
                pltpu.VMEM((n, 3 * half, LANES), f32),
                pltpu.VMEM((n, 3 * half, LANES), f32),
                pltpu.VMEM((n, half, LANES), f32),
                pltpu.VMEM((experts, depth), bf16),
                pltpu.VMEM((n_z, experts, depth), bf16),
                dma((2, 2)), dma((2,)), dma((6, n)), dma((6, n)), dma((n_z,)), dma((n_z,)),
            ],
            compiler_params=pltpu.CompilerParams(
                collective_id=0, has_side_effects=True, vmem_limit_bytes=48 * 2**20
            ),
        )(master_gate, master_up, router_weight.T, router_gain[None, :])
        return (
            og.transpose(1, 2, 0),
            ou.transpose(1, 2, 0),
            osg,
            osu,
            orr.T,
        )

    in_specs = (P("expert", "shard", None), P("expert", "shard", None), P("shard", "expert"), P("shard"))
    out_specs = (P("expert", None, "shard"), P("expert", None, "shard"), P("expert", "shard"), P("expert", "shard"), P())
    return jax.shard_map(local, mesh=mesh, in_specs=in_specs, out_specs=out_specs, check_vma=False)
```

time: 253 us -> 99.6 us (0.39); the launches traced: 250 us -> 99.4 us
  local copies, waits for them, and re-layouts: 106 us -> 6.4 us
  Pallas kernels: 0 us -> 92.3 us
  waiting for transfers between devices: 72.8 us -> 0 us
  starting transfers between devices: 35.9 us -> 0 us
  other arithmetic: 34 us -> 0 us
    pallas_call x0 -> x1, Pallas kernels: none -> 92.3 us  [local(): pl.pallas_call(make_kernel(experts, rows, width, None, cols, n_y, n_x, n_...]
    all_to_all x5 -> x0, waiting for transfers between devices: 72.8 us -> none  [the longest x3 57.2 us: sent_to_all(): return lax.all_to_all(copies, axis, split_axis=0, concat_axis=0, tiled=True)]
    unnamed x10 -> x9, local copies, waits for them, and re-layouts: 54.5 us -> 6.4 us
    all_to_all x5 -> x0, local copies, waits for them, and re-layouts: 41.2 us -> none  [the longest x2 20.6 us: local(): lax.all_to_all(narrow_up, 'shard', split_axis=2, concat_axis=1, tiled=True)]
    all_to_all x5 -> x0, starting transfers between devices: 35.9 us -> none  [the longest x3 20.2 us: sent_to_all(): return lax.all_to_all(copies, axis, split_axis=0, concat_axis=0, tiled=True)]
    unnamed x2 -> x0, other arithmetic: 20.4 us -> none
    reduce_sum x3 -> x0, other arithmetic: 12.8 us -> none  [the longest x1 6.36 us: over_copies(): return jnp.sum(everything, axis=0)]
    broadcast_in_dim x2 -> x0, local copies, waits for them, and re-layouts: 8.39 us -> none  [sent_to_all(): copies = jnp.broadcast_to(array, (lax.axis_size(axis), *array.shape))]
  transfers between devices with their start and end apart: 5 -> 0, of which waited for: 4 -> 0; matrix products, arithmetic and copies ran while one was open for 37% -> 0% of each run, Pallas kernels for 0% -> 0%
where the time goes in v1:
time: 99.6 us; the launch traced here: 99.4 us
  Pallas kernels  92.3 us (93%)
  local copies, waits for them, and re-layouts  6.4 us (6%)
    pallas_call x1, Pallas kernels, local(): pl.pallas_call(make_kernel(experts, rows, width, None, cols, n_y, n_x, n_...  92.3 us
    unnamed x9, local copies, waits for them, and re-layouts  6.4 us

profile of v1, /device:TPU:1, one launch (start us, length us, event | category | flops | bytes accessed | tf_op | source)
XLA Modules:
  0.0 99.4 jit_solution(15644140145133437764)
XLA Ops:
  0.6 0.0 copy-start
  0.6 0.7 copy-done
  1.3 0.0 copy-start.1
  1.3 0.7 copy-done.1
  2.0 92.3 %shard_map.83 = (bf16[44,16,2048]{2,1,0:T(8,128)(2,1)S(1)}, bf16[44,16,2048]{2,1,0:T(8,128)(2,1)S(1)}, f32[16,44]{1,0:T(8,128)S(1)}, f32[16,44]{1,0:T(8,128)S(1)}, bf16[64,2048]{1,0:T(8,128)(2,1)S(1)}) custom-call(f32[16,64,1408]{2,1,0:T(8,128)} %gate.1, f32[16,64,1408]{2,1,0:T(8,128)} %up.1, f32[16,64]{1,0:T(8,128)S(1)} %bitcast.8, f32[1,64]{1,0:T(1,128)S(1)} %bitcast.9), custom_call_target="tpu_custom_call" | custom-call | tf_op jit(solution)/shard_map/pallas_call | solution.py:270
  94.3 1.6 %copy.14 = bf16[16,2048,44]{1,0,2:T(8,128)(2,1)} copy(bf16[16,2048,44]{1,0,2:T(8,128)(2,1)S(1)} %bitcast.6) | data formatting | bytes 5767168
  95.9 1.6 %copy.15 = bf16[16,2048,44]{1,0,2:T(8,128)(2,1)} copy(bf16[16,2048,44]{1,0,2:T(8,128)(2,1)S(1)} %bitcast.5) | data formatting | bytes 5767168
  97.5 0.6 copy.16
  98.1 0.6 copy.17
  98.7 0.7 copy.18
Async XLA Ops:
  0.6 0.7 copy-start
  1.3 0.7 copy-start.1

commit v2 on v0

v2 whole, which is shorter than its diff:
```python
import jax
import jax.numpy as jnp
from jax import lax
from jax.experimental import pallas as pl
from jax.experimental.pallas import tpu as pltpu
from jax.sharding import PartitionSpec as P

MESH = pl.DeviceIdType.MESH
LANES = 128
SUBS = 8
SPAN = 250.0
FLOOR = 124.0
MIX, START = 11, 16
QUARTERS = 4


def encoded(x, partial):
    rate = jnp.where(partial > 0, SPAN * lax.rsqrt(partial), 0.0)
    code = jnp.exp2(jnp.abs(x) * rate - FLOOR)
    return jnp.where(x < 0, -code, code)


def make_kernel(experts, rows, width, cols, n_y, n_x, n_z):
    n = n_y * n_x * 2
    chips = n // 2
    few = experts // QUARTERS
    blocks = width // LANES
    piece = cols * few
    half_lane = LANES // 2

    def kernel(gate, up, router, gain, og, ou, osg, osu, orr,
               xg, xu, stage, code, got, sums, msg, inbox, factor, xr, xgain, rtile, rin, zbuf, zgot,
               in_sem, small_sem, own_sem, send_sem, recv_sem, sums_send, sums_recv, rsend, rrecv, pair_sem, zsend, zrecv):
        me = lax.axis_index("shard")
        plane = lax.axis_index("expert")
        my_chip, my_k = me // 2, me % 2
        my_y, my_x = my_chip // n_x, my_chip % n_x

        def load(a, t):
            src, dst = ((gate, xg), (up, xu))[t]
            return pltpu.make_async_copy(src.at[pl.ds(a * few, few)], dst.at[pl.ds(a * few, few)], in_sem.at[a, t])

        small = [pltpu.make_async_copy(router, xr, small_sem.at[0]), pltpu.make_async_copy(gain, xgain, small_sem.at[1])]
        for t in range(2):
            load(0, t).start()
        for c in small:
            c.start()
        barrier = pltpu.get_barrier_semaphore()
        for d in range(1, n_z):
            pl.semaphore_signal(barrier, 1, device_id={"expert": lax.rem(plane + d, n_z)}, device_id_type=MESH)

        def chip_at(d):
            y = lax.rem(my_y + d // (2 * n_x), n_y)
            x = lax.rem(my_x + (d // 2) % n_x, n_x)
            return y * n_x + x

        order = [d for d in ((i * MIX + START) % n for i in range(n)) if d]
        peers = [chip_at(d) * 2 + lax.rem(my_k + d % 2, 2) for d in order]
        for q in peers:
            pl.semaphore_signal(barrier, 1, device_id={"shard": q}, device_id_type=MESH)
        for a in range(1, QUARTERS):
            for t in range(2):
                load(a, t).start()

        row = lax.broadcasted_iota(jnp.int32, (SUBS, LANES), 0)
        lane = lax.broadcasted_iota(jnp.int32, (SUBS, LANES), 1)
        left = lane < half_lane
        upper = row < few

        def across_lanes(v):
            return pltpu.roll(v, half_lane, axis=1)

        def produce(a):
            h, e0 = a // 2, (a % 2) * few

            def block(b, z):
                at = pl.ds(pl.multiple_of(b * LANES, LANES), LANES)
                for e in range(few):
                    g = xg[a * few + e, :, at]
                    u = xu[a * few + e, :, at]
                    pg = jnp.sum(g * g, axis=0, keepdims=True)
                    pu = jnp.sum(u * u, axis=0, keepdims=True)
                    sums[h, 0, pl.ds(e0 + e, 1), at] = pg
                    sums[h, 1, pl.ds(e0 + e, 1), at] = pu
                    both = jnp.concatenate([encoded(g, pg), encoded(u, pu)], axis=0)
                    stage[pl.ds(e, LANES, stride=few), :] = both.T
                size = LANES * few
                code[a, pl.ds(pl.multiple_of(b * size, size), size), :] = stage[...].astype(jnp.bfloat16)
                return z

            lax.fori_loop(0, blocks, block, 0)

        def message(h):
            def one(q, z):
                first = q * cols
                lo = pl.multiple_of(first // LANES * LANES, LANES)
                s = lax.rem(first, LANES)
                sides = []
                for t, shift in ((0, lax.rem(LANES - s, LANES)), (1, lax.rem(LANES + half_lane - s, LANES))):
                    a = pltpu.roll(sums[h, t, :, pl.ds(lo, LANES)], shift, axis=1)
                    b = pltpu.roll(sums[h, t, :, pl.ds(lo + LANES, LANES)], shift, axis=1)
                    sides.append(jnp.where(lane - t * half_lane + s < LANES, a, b))
                msg[h, q] = jnp.where(left, sides[0], sides[1])
                return z

            lax.fori_loop(0, n, one, 0)
            inbox[h, me] = msg[h, me]

        def piece_to(a, q):
            return pltpu.make_async_remote_copy(
                code.at[a, pl.ds(pl.multiple_of(q * piece, 16), piece)], got.at[a, me],
                send_sem.at[a], recv_sem.at[a, me], device_id={"shard": q}, device_id_type=MESH,
            )

        def piece_from(a, s):
            return pltpu.make_async_remote_copy(
                got.at[a, s], got.at[a, s], send_sem.at[a], recv_sem.at[a, s], device_id={"shard": s}, device_id_type=MESH,
            )

        def all_pieces(a):
            ref = code.at[a, pl.ds(0, (n - 1) * piece)]
            return pltpu.make_async_remote_copy(
                ref, ref, send_sem.at[a], recv_sem.at[a, 0], device_id={"shard": me}, device_id_type=MESH
            )

        def sums_to(h, q):
            return pltpu.make_async_remote_copy(
                msg.at[h, q], inbox.at[h, me], sums_send.at[h], sums_recv.at[h], device_id={"shard": q}, device_id_type=MESH
            )

        def all_sums(h):
            src, dst = msg.at[h, pl.ds(0, n - 1)], inbox.at[h, pl.ds(0, n - 1)]
            return pltpu.make_async_remote_copy(
                src, dst, sums_send.at[h], sums_recv.at[h], device_id={"shard": me}, device_id_type=MESH
            )

        def own(a):
            return pltpu.make_async_copy(
                code.at[a, pl.ds(pl.multiple_of(me * piece, 16), piece)], got.at[a, me], own_sem.at[a]
            )

        def tile_to(q):
            return pltpu.make_async_remote_copy(
                rtile, rin.at[my_k, my_chip], rsend, rrecv, device_id={"shard": q}, device_id_type=MESH
            )

        def all_tiles():
            ref = rin.at[0, pl.ds(0, chips - 1)]
            return pltpu.make_async_remote_copy(ref, ref, rsend, rrecv, device_id={"shard": me}, device_id_type=MESH)

        def to_partner(k):
            return pltpu.make_async_remote_copy(
                rin.at[k], rin.at[k], pair_sem.at[0], pair_sem.at[1],
                device_id={"shard": my_chip * 2 + 1 - my_k}, device_id_type=MESH,
            )

        for a in range(QUARTERS):
            for t in range(2):
                load(a, t).wait()
            produce(a)
            if a == 0:
                for c in small:
                    c.wait()
                folded = xr[...] * xgain[...]
                rtile[...] = jnp.concatenate([folded[:SUBS], folded[SUBS:]], axis=1).astype(jnp.bfloat16)
                rin[my_k, my_chip] = rtile[...]
                pl.semaphore_wait(barrier, n - 1 + n_z - 1)
            if a % 2:
                message(a // 2)
                for q in peers:
                    sums_to(a // 2, q).start()
            for q in peers:
                piece_to(a, q).start()
            own(a).start()
            if a == 0:
                for d, q in zip(order, peers):
                    if d % 2 == 0:
                        tile_to(q).start()

        all_tiles().wait_recv()
        to_partner(my_k).start()
        to_partner(1 - my_k).wait_recv()

        def join(c, z):
            a, b = rin[0, c].astype(jnp.float32), rin[1, c].astype(jnp.float32)
            low = jnp.where(left, a, across_lanes(b))
            high = jnp.where(left, across_lanes(a), b)
            zbuf[:, pl.ds(pl.multiple_of(c * LANES, LANES), LANES)] = jnp.concatenate([low, high], axis=0).astype(jnp.bfloat16)
            return z

        lax.fori_loop(0, chips, join, 0)

        def across(d, slot):
            z = lax.rem(plane + d, n_z)
            return pltpu.make_async_remote_copy(
                zbuf, zgot.at[slot], zsend.at[d], zrecv.at[slot], device_id={"expert": z}, device_id_type=MESH
            )

        for d in range(1, n_z):
            across(d, plane).start()
        orr[pl.ds(pl.multiple_of(plane * experts, experts), experts), :] = zbuf[...]

        def factors(h):
            all_sums(h).wait_recv()
            total = lax.fori_loop(0, n, lambda s, t: t + inbox[h, s], jnp.zeros((SUBS, LANES), jnp.float32))
            scale = jnp.sqrt(total)
            osg[pl.ds(h * SUBS, SUBS), :] = scale[:, :cols]
            osu[pl.ds(h * SUBS, SUBS), :] = across_lanes(scale)[:, :cols]
            share = 1.0 / (SPAN * scale)

            def one(s, z):
                f = jnp.sqrt(inbox[h, s]) * share
                r = pltpu.roll(f, few, axis=0)
                factor[s, 0] = jnp.where(upper, f, r)
                factor[s, 1] = jnp.where(upper, r, f)
                return z

            lax.fori_loop(0, n, one, 0)

        pick = jnp.where(left, 0, half_lane) + jnp.where(upper, 0, 1)

        def decode(h):
            def chip(i, z):
                dc = lax.rem(START // 2 + MIX * i, chips)
                y = lax.rem(my_y - dc // n_x + n_y, n_y)
                x = lax.rem(my_x - dc % n_x + n_x, n_x)
                at = y * n_x + x
                for k in range(2):
                    @pl.when(2 * at + k != me)
                    def arrival():
                        for b in range(2):
                            piece_from(2 * h + b, 2 * at + k).wait_recv()

                lanes_out = pl.ds(pl.multiple_of(at * LANES, LANES), LANES)

                def values(b, k, p):
                    v = got[2 * h + b, 2 * at + k, pl.ds(p * 16, 16), :].astype(jnp.float32)
                    f = factor[2 * at + k, b]
                    out = []
                    for r in range(2):
                        w = v[r * SUBS:(r + 1) * SUBS]
                        mul = jnp.take_along_axis(f, pick + (4 * p + 2 * r), axis=1)
                        x = (jnp.log2(jnp.abs(w)) + FLOOR) * mul
                        out.append(jnp.where(w < 0, -x, x))
                    return out

                for p in range(cols // 4):
                    parts = []
                    for b in range(2):
                        one, two = values(b, 0, p), values(b, 1, p)
                        sides = []
                        for r in range(2):
                            turned = across_lanes(jnp.where(left, two[r], one[r]))
                            sides.append((jnp.where(left, one[r], turned), jnp.where(left, turned, two[r])))
                        parts.append(sides)
                    for r in range(2):
                        for t, out in ((0, og), (1, ou)):
                            a, b = parts[0][r][t], parts[1][r][t]
                            turned = pltpu.roll(jnp.where(upper, b, a), few, axis=0)
                            j = 4 * p + 2 * r
                            out[j, pl.ds(h * SUBS, SUBS), lanes_out] = jnp.where(upper, a, turned).astype(jnp.bfloat16)
                            out[j + 1, pl.ds(h * SUBS, SUBS), lanes_out] = jnp.where(upper, turned, b).astype(jnp.bfloat16)
                return z

            lax.fori_loop(0, chips, chip, 0)

        for h in range(2):
            factors(h)
            for b in range(2):
                own(2 * h + b).wait()
            decode(h)

        for d in range(1, n_z):
            z = lax.rem(plane + d, n_z)
            across(d, plane).wait_send()
            across(d, z).wait_recv()
            orr[pl.ds(pl.multiple_of(z * experts, experts), experts), :] = zgot[z]
        to_partner(my_k).wait_send()
        all_tiles().wait_send()
        for h in range(2):
            all_sums(h).wait_send()
        for a in range(QUARTERS):
            all_pieces(a).wait_send()

    return kernel


def in_hbm(array):
    return pltpu.with_memory_space_constraint(array, pltpu.HBM)


def put_out(*refs):
    n = len(refs) // 2
    sems = refs[-1]
    copies = [pltpu.make_async_copy(refs[i], refs[n + i], sems.at[i]) for i in range(n)]
    for c in copies:
        c.start()
    for c in copies:
        c.wait()


def solution(mesh):
    n_z, n = mesh.shape["expert"], mesh.shape["shard"]
    n_y = n_x = 4

    def local(master_gate, master_up, router_weight, router_gain):
        experts, rows, width = master_gate.shape
        cols = width // n
        depth = rows * n
        few = experts // QUARTERS
        f32, bf16 = jnp.float32, jnp.bfloat16
        vmem = pl.BlockSpec(memory_space=pltpu.VMEM)
        hbm = pl.BlockSpec(memory_space=pltpu.HBM)
        dma = pltpu.SemaphoreType.DMA
        shapes = (
            jax.ShapeDtypeStruct((cols, experts, depth), bf16),
            jax.ShapeDtypeStruct((cols, experts, depth), bf16),
            jax.ShapeDtypeStruct((experts, cols), f32),
            jax.ShapeDtypeStruct((experts, cols), f32),
            jax.ShapeDtypeStruct((experts * n_z, depth), bf16),
        )
        results = pl.pallas_call(
            make_kernel(experts, rows, width, cols, n_y, n_x, n_z),
            out_shape=shapes,
            in_specs=[hbm] * 4,
            out_specs=(vmem,) * 5,
            scratch_shapes=[
                pltpu.VMEM((experts, rows, width), f32),
                pltpu.VMEM((experts, rows, width), f32),
                pltpu.VMEM((LANES * few, LANES), f32),
                pltpu.VMEM((QUARTERS, width * few, LANES), bf16),
                pltpu.VMEM((QUARTERS, n, cols * few, LANES), bf16),
                pltpu.VMEM((2, 2, SUBS, width + LANES), f32),
                pltpu.VMEM((2, n, SUBS, LANES), f32),
                pltpu.VMEM((2, n, SUBS, LANES), f32),
                pltpu.VMEM((n, 2, SUBS, LANES), f32),
                pltpu.VMEM((experts, rows), f32),
                pltpu.VMEM((1, rows), f32),
                pltpu.VMEM((SUBS, LANES), bf16),
                pltpu.VMEM((2, n // 2, SUBS, LANES), bf16),
                pltpu.VMEM((experts, depth), bf16),
                pltpu.VMEM((n_z, experts, depth), bf16),
                dma((QUARTERS, 2)), dma((2,)), dma((QUARTERS,)), dma((QUARTERS,)), dma((QUARTERS, n)), dma((2,)), dma((2,)),
                dma, dma, dma((2,)), dma((n_z,)), dma((n_z,)),
            ],
            compiler_params=pltpu.CompilerParams(
                collective_id=0, has_side_effects=True, vmem_limit_bytes=48 * 2**20
            ),
        )(master_gate, master_up, in_hbm(router_weight.T), in_hbm(router_gain[None, :]))
        og, ou, osg, osu, orr = pl.pallas_call(
            put_out,
            out_shape=shapes,
            in_specs=[pl.BlockSpec(memory_space=pl.ANY)] * 5,
            out_specs=(hbm,) * 5,
            scratch_shapes=[dma((5,))],
            compiler_params=pltpu.CompilerParams(vmem_limit_bytes=2**20),
        )(*results)
        return og.transpose(1, 2, 0), ou.transpose(1, 2, 0), osg, osu, orr.T

    in_specs = (P("expert", "shard", None), P("expert", "shard", None), P("shard", "expert"), P("shard"))
    out_specs = (P("expert", None, "shard"), P("expert", None, "shard"), P("expert", "shard"), P("expert", "shard"), P())
    return jax.shard_map(local, mesh=mesh, in_specs=in_specs, out_specs=out_specs, check_vma=False)
```

time: 253 us -> 84.8 us (0.34)
  local copies, waits for them, and re-layouts: 106 us -> 0 us
  Pallas kernels: 0 us -> 82.8 us
  waiting for transfers between devices: 72.8 us -> 0 us
  starting transfers between devices: 35.9 us -> 0 us
  other arithmetic: 34 us -> 0 us
    pallas_call x0 -> x2, Pallas kernels: none -> 82.8 us  [the longest x1 80.1 us: local(): pl.pallas_call(make_kernel(experts, rows, width, cols, n_y, n_x, n_z), ou...]
    all_to_all x5 -> x0, waiting for transfers between devices: 72.8 us -> none  [the longest x3 57.2 us: sent_to_all(): return lax.all_to_all(copies, axis, split_axis=0, concat_axis=0, tiled=True)]
    unnamed x10 -> x0, local copies, waits for them, and re-layouts: 54.5 us -> none
    all_to_all x5 -> x0, local copies, waits for them, and re-layouts: 41.2 us -> none  [the longest x2 20.6 us: local(): lax.all_to_all(narrow_up, 'shard', split_axis=2, concat_axis=1, tiled=True)]
    all_to_all x5 -> x0, starting transfers between devices: 35.9 us -> none  [the longest x3 20.2 us: sent_to_all(): return lax.all_to_all(copies, axis, split_axis=0, concat_axis=0, tiled=True)]
    unnamed x2 -> x0, other arithmetic: 20.4 us -> none
    reduce_sum x3 -> x0, other arithmetic: 12.8 us -> none  [the longest x1 6.36 us: over_copies(): return jnp.sum(everything, axis=0)]
    broadcast_in_dim x2 -> x0, local copies, waits for them, and re-layouts: 8.39 us -> none  [sent_to_all(): copies = jnp.broadcast_to(array, (lax.axis_size(axis), *array.shape))]
  transfers between devices with their start and end apart: 5 -> 0, of which waited for: 4 -> 0; matrix products, arithmetic and copies ran while one was open for 37% -> 0% of each run, Pallas kernels for 0% -> 0%
where the time goes in v2:
time: 84.8 us; the launch traced here: 83.4 us
  Pallas kernels  82.8 us (98%)
    pallas_call x1, Pallas kernels, local(): pl.pallas_call(make_kernel(experts, rows, width, cols, n_y, n_x, n_z), ou...  80.1 us
    pallas_call x1, Pallas kernels, local(): pl.pallas_call(put_out, out_shape=shapes, in_specs=[pl.BlockSpec(memory_s...  2.66 us

profile of v2, /device:TPU:1, one launch (start us, length us, event | category | flops | bytes accessed | tf_op | source)
XLA Modules:
  0.0 83.4 jit_solution(4030661831106272860)
XLA Ops:
  0.6 80.1 %shard_map.83 = (bf16[44,16,2048]{2,1,0:T(8,128)(2,1)S(1)}, bf16[44,16,2048]{2,1,0:T(8,128)(2,1)S(1)}, f32[16,44]{1,0:T(8,128)S(1)}, f32[16,44]{1,0:T(8,128)S(1)}, bf16[64,2048]{1,0:T(8,128)(2,1)S(1)}) custom-call(f32[16,64,1408]{2,1,0:T(8,128)} %gate.1, f32[16,64,1408]{2,1,0:T(8,128)} %up.1, f32[16,64]{1,0:T(8,128)} %bitcast.5, f32[1,64]{1,0:T(1,128)} %bitcast.6), custom_call_target="tpu_custom_call" | custom-call | tf_op jit(solution)/shard_map/pallas_call | solution.py:322
  80.7 2.7 %shard_map.84 = (bf16[44,16,2048]{2,1,0:T(8,128)(2,1)}, bf16[44,16,2048]{2,1,0:T(8,128)(2,1)}, f32[16,44]{1,0:T(8,128)}, f32[16,44]{1,0:T(8,128)}, bf16[64,2048]{1,0:T(8,128)(2,1)}) custom-call(bf16[44,16,2048]{2,1,0:T(8,128)(2,1)S(1)} %get-tuple-element.15.refs_0_, bf16[44,16,2048]{2,1,0:T(8,128)(2,1)S(1)} %get-tuple-element.16.refs_1_, ...), custom_call_target="tpu_custom_call" | custom-call | tf_op jit(solution)/shard_map/pallas_call | solution.py:350

commit v3 on v2

--- a/solution.py
+++ b/solution.py
@@ -11,7 +11,7 @@
 SPAN = 250.0
 FLOOR = 124.0
 MIX, START = 11, 16
-QUARTERS = 4
+PARTS = (24, 20)
 
 
 def encoded(x, partial):
@@ -23,22 +23,28 @@
 def make_kernel(experts, rows, width, cols, n_y, n_x, n_z):
     n = n_y * n_x * 2
     chips = n // 2
-    few = experts // QUARTERS
+    few = SUBS // 2
     blocks = width // LANES
-    piece = cols * few
     half_lane = LANES // 2
+    pieces = [(0, 0, cols * few), (1, 0, cols * few)]
+    for i in range(len(PARTS)):
+        pieces.append((2, sum(PARTS[:i]) * SUBS, PARTS[i] * SUBS))
 
     def kernel(gate, up, router, gain, og, ou, osg, osu, orr,
-               xg, xu, stage, code, got, sums, msg, inbox, factor, xr, xgain, rtile, rin, zbuf, zgot,
+               xg, xu, stage, code_a, code_b, code_c, got_a, got_b, got_c, sums, msg, inbox, share, spread,
+               xr, xgain, rtile, rin, zbuf, zgot,
                in_sem, small_sem, own_sem, send_sem, recv_sem, sums_send, sums_recv, rsend, rrecv, pair_sem, zsend, zrecv):
+        codes, gots = (code_a, code_b, code_c), (got_a, got_b, got_c)
         me = lax.axis_index("shard")
         plane = lax.axis_index("expert")
         my_chip, my_k = me // 2, me % 2
         my_y, my_x = my_chip // n_x, my_chip % n_x
+        stretches = ((0, few), (few, few), (2 * few, SUBS))
 
         def load(a, t):
             src, dst = ((gate, xg), (up, xu))[t]
-            return pltpu.make_async_copy(src.at[pl.ds(a * few, few)], dst.at[pl.ds(a * few, few)], in_sem.at[a, t])
+            at = pl.ds(*stretches[a])
+            return pltpu.make_async_copy(src.at[at], dst.at[at], in_sem.at[a, t])
 
         small = [pltpu.make_async_copy(router, xr, small_sem.at[0]), pltpu.make_async_copy(gain, xgain, small_sem.at[1])]
         for t in range(2):
@@ -58,34 +64,37 @@
         peers = [chip_at(d) * 2 + lax.rem(my_k + d % 2, 2) for d in order]
         for q in peers:
             pl.semaphore_signal(barrier, 1, device_id={"shard": q}, device_id_type=MESH)
-        for a in range(1, QUARTERS):
+        for a in range(1, 3):
             for t in range(2):
                 load(a, t).start()
 
         row = lax.broadcasted_iota(jnp.int32, (SUBS, LANES), 0)
         lane = lax.broadcasted_iota(jnp.int32, (SUBS, LANES), 1)
         left = lane < half_lane
+        left2 = lax.broadcasted_iota(jnp.int32, (2 * SUBS, LANES), 1) < half_lane
         upper = row < few
+        used = lax.rem(lane, half_lane) < cols
 
         def across_lanes(v):
             return pltpu.roll(v, half_lane, axis=1)
 
         def produce(a):
-            h, e0 = a // 2, (a % 2) * few
+            first, count = stretches[a]
+            h, e0 = first // SUBS, first % SUBS
+            size = LANES * count
 
             def block(b, z):
                 at = pl.ds(pl.multiple_of(b * LANES, LANES), LANES)
-                for e in range(few):
-                    g = xg[a * few + e, :, at]
-                    u = xu[a * few + e, :, at]
+                for e in range(count):
+                    g = xg[first + e, :, at]
+                    u = xu[first + e, :, at]
                     pg = jnp.sum(g * g, axis=0, keepdims=True)
                     pu = jnp.sum(u * u, axis=0, keepdims=True)
                     sums[h, 0, pl.ds(e0 + e, 1), at] = pg
                     sums[h, 1, pl.ds(e0 + e, 1), at] = pu
                     both = jnp.concatenate([encoded(g, pg), encoded(u, pu)], axis=0)
-                    stage[pl.ds(e, LANES, stride=few), :] = both.T
-                size = LANES * few
-                code[a, pl.ds(pl.multiple_of(b * size, size), size), :] = stage[...].astype(jnp.bfloat16)
+                    stage[pl.ds(e, LANES, stride=count), :] = both.T
+                codes[a][pl.ds(pl.multiple_of(b * size, size), size), :] = stage[pl.ds(0, size), :].astype(jnp.bfloat16)
                 return z
 
             lax.fori_loop(0, blocks, block, 0)
@@ -106,21 +115,26 @@
             lax.fori_loop(0, n, one, 0)
             inbox[h, me] = msg[h, me]
 
-        def piece_to(a, q):
-            return pltpu.make_async_remote_copy(
-                code.at[a, pl.ds(pl.multiple_of(q * piece, 16), piece)], got.at[a, me],
-                send_sem.at[a], recv_sem.at[a, me], device_id={"shard": q}, device_id_type=MESH,
-            )
-
-        def piece_from(a, s):
-            return pltpu.make_async_remote_copy(
-                got.at[a, s], got.at[a, s], send_sem.at[a], recv_sem.at[a, s], device_id={"shard": s}, device_id_type=MESH,
-            )
-
-        def all_pieces(a):
-            ref = code.at[a, pl.ds(0, (n - 1) * piece)]
-            return pltpu.make_async_remote_copy(
-                ref, ref, send_sem.at[a], recv_sem.at[a, 0], device_id={"shard": me}, device_id_type=MESH
+        def piece_to(m, q):
+            a, first, size = pieces[m]
+            whole = cols * stretches[a][1]
+            return pltpu.make_async_remote_copy(
+                codes[a].at[pl.ds(pl.multiple_of(q * whole + first, 16), size)], gots[a].at[me, pl.ds(first, size)],
+                send_sem.at[m], recv_sem.at[m, me], device_id={"shard": q}, device_id_type=MESH,
+            )
+
+        def piece_from(m, s):
+            a, first, size = pieces[m]
+            ref = gots[a].at[s, pl.ds(first, size)]
+            return pltpu.make_async_remote_copy(
+                ref, ref, send_sem.at[m], recv_sem.at[m, s], device_id={"shard": s}, device_id_type=MESH
+            )
+
+        def all_pieces(m):
+            a, _, size = pieces[m]
+            ref = codes[a].at[pl.ds(0, (n - 1) * size)]
+            return pltpu.make_async_remote_copy(
+                ref, ref, send_sem.at[m], recv_sem.at[m, 0], device_id={"shard": me}, device_id_type=MESH
             )
 
         def sums_to(h, q):
@@ -135,8 +149,9 @@
             )
 
         def own(a):
+            size = cols * stretches[a][1]
             return pltpu.make_async_copy(
-                code.at[a, pl.ds(pl.multiple_of(me * piece, 16), piece)], got.at[a, me], own_sem.at[a]
+                codes[a].at[pl.ds(pl.multiple_of(me * size, 16), size)], gots[a].at[me], own_sem.at[a]
             )
 
         def tile_to(q):
@@ -154,7 +169,7 @@
                 device_id={"shard": my_chip * 2 + 1 - my_k}, device_id_type=MESH,
             )
 
-        for a in range(QUARTERS):
+        for a in range(3):
             for t in range(2):
                 load(a, t).wait()
             produce(a)
@@ -165,12 +180,14 @@
                 rtile[...] = jnp.concatenate([folded[:SUBS], folded[SUBS:]], axis=1).astype(jnp.bfloat16)
                 rin[my_k, my_chip] = rtile[...]
                 pl.semaphore_wait(barrier, n - 1 + n_z - 1)
-            if a % 2:
-                message(a // 2)
+            else:
+                message(a - 1)
                 for q in peers:
-                    sums_to(a // 2, q).start()
-            for q in peers:
-                piece_to(a, q).start()
+                    sums_to(a - 1, q).start()
+            for m in range(len(pieces)):
+                if pieces[m][0] == a:
+                    for q in peers:
+                        piece_to(m, q).start()
             own(a).start()
             if a == 0:
                 for d, q in zip(order, peers):
@@ -206,20 +223,47 @@
             scale = jnp.sqrt(total)
             osg[pl.ds(h * SUBS, SUBS), :] = scale[:, :cols]
             osu[pl.ds(h * SUBS, SUBS), :] = across_lanes(scale)[:, :cols]
-            share = 1.0 / (SPAN * scale)
-
-            def one(s, z):
-                f = jnp.sqrt(inbox[h, s]) * share
-                r = pltpu.roll(f, few, axis=0)
-                factor[s, 0] = jnp.where(upper, f, r)
-                factor[s, 1] = jnp.where(upper, r, f)
+            each = 1.0 / (SPAN * scale)
+            some = jnp.logical_and(used, total > 0)
+
+            def one(c, z):
+                a = jnp.where(some, jnp.sqrt(inbox[h, 2 * c]) * each, 0.0)
+                b = jnp.where(some, jnp.sqrt(inbox[h, 2 * c + 1]) * each, 0.0)
+                turned = across_lanes(jnp.where(left, b, a))
+                for t, f in ((0, jnp.where(left, a, turned)), (1, jnp.where(left, turned, b))):
+                    at = pl.ds(pl.multiple_of(t * chips * SUBS + c * SUBS, SUBS), SUBS)
+                    high = f.astype(jnp.bfloat16).astype(jnp.float32)
+                    share[at, pl.ds(0, LANES)] = high
+                    share[at, pl.ds(LANES, LANES)] = f - high
                 return z
 
-            lax.fori_loop(0, n, one, 0)
-
-        pick = jnp.where(left, 0, half_lane) + jnp.where(upper, 0, 1)
-
-        def decode(h):
+            lax.fori_loop(0, chips, one, 0)
+            lhs = share[...].astype(jnp.bfloat16)
+            k = lax.rem(lax.broadcasted_iota(jnp.int32, (2 * LANES, 2 * LANES), 0), LANES)
+            m = lax.broadcasted_iota(jnp.int32, (2 * LANES, 2 * LANES), 1)
+            source = k - m // LANES - lax.rem(m, LANES) // half_lane * half_lane
+
+            def two(p, z):
+                pick = jnp.where(source == 2 * p, 1.0, 0.0).astype(jnp.bfloat16)
+                wide = jnp.dot(lhs, pick, preferred_element_type=jnp.float32)
+                spread[2 * p] = wide[:, :LANES]
+                spread[2 * p + 1] = wide[:, LANES:]
+                return z
+
+            lax.fori_loop(0, cols // 2, two, 0)
+
+        def exponents(v):
+            v = v.astype(jnp.float32)
+            x = jnp.log2(jnp.abs(v)) + FLOOR
+            return jnp.where(v < 0, -x, x)
+
+        def merged(one, two):
+            turned = across_lanes(jnp.where(left2, two, one))
+            return jnp.where(left2, one, turned), jnp.where(left2, turned, two)
+
+        def decode(ms, first, count):
+            h = 0 if pieces[ms[0]][0] < 2 else 1
+
             def chip(i, z):
                 dc = lax.rem(START // 2 + MIX * i, chips)
                 y = lax.rem(my_y - dc // n_x + n_y, n_y)
@@ -228,47 +272,44 @@
                 for k in range(2):
                     @pl.when(2 * at + k != me)
                     def arrival():
-                        for b in range(2):
-                            piece_from(2 * h + b, 2 * at + k).wait_recv()
+                        for m in ms:
+                            piece_from(m, 2 * at + k).wait_recv()
 
                 lanes_out = pl.ds(pl.multiple_of(at * LANES, LANES), LANES)
 
-                def values(b, k, p):
-                    v = got[2 * h + b, 2 * at + k, pl.ds(p * 16, 16), :].astype(jnp.float32)
-                    f = factor[2 * at + k, b]
-                    out = []
-                    for r in range(2):
-                        w = v[r * SUBS:(r + 1) * SUBS]
-                        mul = jnp.take_along_axis(f, pick + (4 * p + 2 * r), axis=1)
-                        x = (jnp.log2(jnp.abs(w)) + FLOOR) * mul
-                        out.append(jnp.where(w < 0, -x, x))
-                    return out
-
-                for p in range(cols // 4):
-                    parts = []
-                    for b in range(2):
-                        one, two = values(b, 0, p), values(b, 1, p)
-                        sides = []
-                        for r in range(2):
-                            turned = across_lanes(jnp.where(left, two[r], one[r]))
-                            sides.append((jnp.where(left, one[r], turned), jnp.where(left, turned, two[r])))
-                        parts.append(sides)
-                    for r in range(2):
-                        for t, out in ((0, og), (1, ou)):
-                            a, b = parts[0][r][t], parts[1][r][t]
-                            turned = pltpu.roll(jnp.where(upper, b, a), few, axis=0)
-                            j = 4 * p + 2 * r
-                            out[j, pl.ds(h * SUBS, SUBS), lanes_out] = jnp.where(upper, a, turned).astype(jnp.bfloat16)
-                            out[j + 1, pl.ds(h * SUBS, SUBS), lanes_out] = jnp.where(upper, turned, b).astype(jnp.bfloat16)
+                def put(t, j, x):
+                    f = spread[j, pl.ds(pl.multiple_of(t * chips * SUBS + at * SUBS, SUBS), SUBS), :]
+                    (og, ou)[t][j, pl.ds(h * SUBS, SUBS), lanes_out] = (x * f).astype(jnp.bfloat16)
+
+                if h:
+                    for j in range(first, first + count, 2):
+                        sides = merged(*(exponents(got_c[2 * at + k, pl.ds(j * SUBS, 2 * SUBS), :]) for k in range(2)))
+                        for t in range(2):
+                            for r in range(2):
+                                put(t, j + r, sides[t][r * SUBS:(r + 1) * SUBS])
+                else:
+                    for j in range(first, first + count, 4):
+                        rng = pl.ds(j * few, 2 * SUBS)
+                        one = merged(*(exponents(got_a[2 * at + k, rng, :]) for k in range(2)))
+                        two = merged(*(exponents(got_b[2 * at + k, rng, :]) for k in range(2)))
+                        for t in range(2):
+                            for r in range(2):
+                                a, b = one[t][r * SUBS:(r + 1) * SUBS], two[t][r * SUBS:(r + 1) * SUBS]
+                                turned = pltpu.roll(jnp.where(upper, b, a), few, axis=0)
+                                put(t, j + 2 * r, jnp.where(upper, a, turned))
+                                put(t, j + 2 * r + 1, jnp.where(upper, turned, b))
                 return z
 
             lax.fori_loop(0, chips, chip, 0)
 
-        for h in range(2):
-            factors(h)
-            for b in range(2):
-                own(2 * h + b).wait()
-            decode(h)
+        factors(0)
+        own(0).wait()
+        own(1).wait()
+        decode((0, 1), 0, cols)
+        factors(1)
+        own(2).wait()
+        for i in range(len(PARTS)):
+            decode((2 + i,), sum(PARTS[:i]), PARTS[i])
 
         for d in range(1, n_z):
             z = lax.rem(plane + d, n_z)
@@ -279,8 +320,8 @@
         all_tiles().wait_send()
         for h in range(2):
             all_sums(h).wait_send()
-        for a in range(QUARTERS):
-            all_pieces(a).wait_send()
+        for m in range(len(pieces)):
+            all_pieces(m).wait_send()
 
     return kernel
 
@@ -307,7 +348,8 @@
         experts, rows, width = master_gate.shape
         cols = width // n
         depth = rows * n
-        few = experts // QUARTERS
+        few = SUBS // 2
+        sent = 2 + len(PARTS)
         f32, bf16 = jnp.float32, jnp.bfloat16
         vmem = pl.BlockSpec(memory_space=pltpu.VMEM)
         hbm = pl.BlockSpec(memory_space=pltpu.HBM)
@@ -327,20 +369,25 @@
             scratch_shapes=[
                 pltpu.VMEM((experts, rows, width), f32),
                 pltpu.VMEM((experts, rows, width), f32),
-                pltpu.VMEM((LANES * few, LANES), f32),
-                pltpu.VMEM((QUARTERS, width * few, LANES), bf16),
-                pltpu.VMEM((QUARTERS, n, cols * few, LANES), bf16),
+                pltpu.VMEM((LANES * SUBS, LANES), f32),
+                pltpu.VMEM((width * few, LANES), bf16),
+                pltpu.VMEM((width * few, LANES), bf16),
+                pltpu.VMEM((width * SUBS, LANES), bf16),
+                pltpu.VMEM((n, cols * few, LANES), bf16),
+                pltpu.VMEM((n, cols * few, LANES), bf16),
+                pltpu.VMEM((n, cols * SUBS, LANES), bf16),
                 pltpu.VMEM((2, 2, SUBS, width + LANES), f32),
                 pltpu.VMEM((2, n, SUBS, LANES), f32),
                 pltpu.VMEM((2, n, SUBS, LANES), f32),
-                pltpu.VMEM((n, 2, SUBS, LANES), f32),
+                pltpu.VMEM((n * SUBS, 2 * LANES), f32),
+                pltpu.VMEM((cols, n * SUBS, LANES), f32),
                 pltpu.VMEM((experts, rows), f32),
                 pltpu.VMEM((1, rows), f32),
                 pltpu.VMEM((SUBS, LANES), bf16),
                 pltpu.VMEM((2, n // 2, SUBS, LANES), bf16),
                 pltpu.VMEM((experts, depth), bf16),
                 pltpu.VMEM((n_z, experts, depth), bf16),
-                dma((QUARTERS, 2)), dma((2,)), dma((QUARTERS,)), dma((QUARTERS,)), dma((QUARTERS, n)), dma((2,)), dma((2,)),
+                dma((3, 2)), dma((2,)), dma((3,)), dma((sent,)), dma((sent, n)), dma((2,)), dma((2,)),
                 dma, dma, dma((2,)), dma((n_z,)), dma((n_z,)),
             ],
             compiler_params=pltpu.CompilerParams(

time: 84.8 us -> 82.1 us (0.968); the launches traced: 83.4 us -> 82 us
  Pallas kernels: 82.8 us -> 81.3 us
    pallas_call x1, Pallas kernels: 80.1 us -> 78.7 us  [local(): pl.pallas_call(make_kernel(experts, rows, width, cols, n_y, n_x, n_z), ou...]
where the time goes in v3:
time: 82.1 us; the launch traced here: 82 us
  Pallas kernels  81.3 us (99%)
    pallas_call x1, Pallas kernels, local(): pl.pallas_call(make_kernel(experts, rows, width, cols, n_y, n_x, n_z), ou...  78.7 us
    pallas_call x1, Pallas kernels, local(): pl.pallas_call(put_out, out_shape=shapes, in_specs=[pl.BlockSpec(memory_s...  2.66 us

profile of v3, /device:TPU:1, one launch (start us, length us, event | category | flops | bytes accessed | tf_op | source)
XLA Modules:
  0.0 82.0 jit_solution(3416948322852546228)
XLA Ops:
  0.6 78.7 %shard_map.83 = (bf16[44,16,2048]{2,1,0:T(8,128)(2,1)S(1)}, bf16[44,16,2048]{2,1,0:T(8,128)(2,1)S(1)}, f32[16,44]{1,0:T(8,128)S(1)}, f32[16,44]{1,0:T(8,128)S(1)}, bf16[64,2048]{1,0:T(8,128)(2,1)S(1)}) custom-call(f32[16,64,1408]{2,1,0:T(8,128)} %gate.1, f32[16,64,1408]{2,1,0:T(8,128)} %up.1, f32[16,64]{1,0:T(8,128)} %bitcast.5, f32[1,64]{1,0:T(1,128)} %bitcast.6), custom_call_target="tpu_custom_call" | custom-call | tf_op jit(solution)/shard_map/pallas_call | solution.py:364
  79.3 2.7 %shard_map.84 = (bf16[44,16,2048]{2,1,0:T(8,128)(2,1)}, bf16[44,16,2048]{2,1,0:T(8,128)(2,1)}, f32[16,44]{1,0:T(8,128)}, f32[16,44]{1,0:T(8,128)}, bf16[64,2048]{1,0:T(8,128)(2,1)}) custom-call(bf16[44,16,2048]{2,1,0:T(8,128)(2,1)S(1)} %get-tuple-element.15.refs_0_, bf16[44,16,2048]{2,1,0:T(8,128)(2,1)S(1)} %get-tuple-element.16.refs_1_, ...), custom_call_target="tpu_custom_call" | custom-call | tf_op jit(solution)/shard_map/pallas_call | solution.py:397

commit v4 on v3

--- a/solution.py
+++ b/solution.py
@@ -26,14 +26,15 @@
     few = SUBS // 2
     blocks = width // LANES
     half_lane = LANES // 2
-    pieces = [(0, 0, cols * few), (1, 0, cols * few)]
+    tile = 2 * SUBS
+    pieces = [(0, 0, cols * few), (1, 0, cols * few + 2 * tile)]
     for i in range(len(PARTS)):
         pieces.append((2, sum(PARTS[:i]) * SUBS, PARTS[i] * SUBS))
 
     def kernel(gate, up, router, gain, og, ou, osg, osu, orr,
-               xg, xu, stage, code_a, code_b, code_c, got_a, got_b, got_c, sums, msg, inbox, share, spread,
+               xg, xu, stage, code_a, code_b, code_c, got_a, got_b, got_c, sums, share, spread,
                xr, xgain, rtile, rin, zbuf, zgot,
-               in_sem, small_sem, own_sem, send_sem, recv_sem, sums_send, sums_recv, rsend, rrecv, pair_sem, zsend, zrecv):
+               in_sem, small_sem, own_sem, send_sem, recv_sem, rsend, rrecv, pair_sem, zsend, zrecv):
         codes, gots = (code_a, code_b, code_c), (got_a, got_b, got_c)
         me = lax.axis_index("shard")
         plane = lax.axis_index("expert")
@@ -47,23 +48,29 @@
             return pltpu.make_async_copy(src.at[at], dst.at[at], in_sem.at[a, t])
 
         small = [pltpu.make_async_copy(router, xr, small_sem.at[0]), pltpu.make_async_copy(gain, xgain, small_sem.at[1])]
-        for t in range(2):
-            load(0, t).start()
-        for c in small:
-            c.start()
-        barrier = pltpu.get_barrier_semaphore()
-        for d in range(1, n_z):
-            pl.semaphore_signal(barrier, 1, device_id={"expert": lax.rem(plane + d, n_z)}, device_id_type=MESH)
-
         def chip_at(d):
             y = lax.rem(my_y + d // (2 * n_x), n_y)
             x = lax.rem(my_x + (d // 2) % n_x, n_x)
             return y * n_x + x
 
+        def hops(d):
+            y, x = d // (2 * n_x), (d // 2) % n_x
+            return min(y, n_y - y) + min(x, n_x - x)
+
         order = [d for d in ((i * MIX + START) % n for i in range(n)) if d]
         peers = [chip_at(d) * 2 + lax.rem(my_k + d % 2, 2) for d in order]
-        for q in peers:
-            pl.semaphore_signal(barrier, 1, device_id={"shard": q}, device_id_type=MESH)
+        barrier = pltpu.get_barrier_semaphore()
+        for far in range(n_y // 2 + n_x // 2, -1, -1):
+            for d, q in zip(order, peers):
+                if hops(d) == far:
+                    pl.semaphore_signal(barrier, 1, device_id={"shard": q}, device_id_type=MESH)
+            if far == 4:
+                for t in range(2):
+                    load(0, t).start()
+        for d in range(1, n_z):
+            pl.semaphore_signal(barrier, 1, device_id={"expert": lax.rem(plane + d, n_z)}, device_id_type=MESH)
+        for c in small:
+            c.start()
         for a in range(1, 3):
             for t in range(2):
                 load(a, t).start()
@@ -93,33 +100,47 @@
                     sums[h, 0, pl.ds(e0 + e, 1), at] = pg
                     sums[h, 1, pl.ds(e0 + e, 1), at] = pu
                     both = jnp.concatenate([encoded(g, pg), encoded(u, pu)], axis=0)
-                    stage[pl.ds(e, LANES, stride=count), :] = both.T
-                codes[a][pl.ds(pl.multiple_of(b * size, size), size), :] = stage[pl.ds(0, size), :].astype(jnp.bfloat16)
+                    stage[pl.ds(pl.multiple_of(b * size, size) + e, LANES, stride=count), :] = both.T
                 return z
 
             lax.fori_loop(0, blocks, block, 0)
-
-        def message(h):
+            own_rows = cols * count
+
+            def pack(q, z):
+                rows_q = stage[pl.ds(pl.multiple_of(q * own_rows, 16), own_rows), :]
+                codes[a][q, pl.ds(0, own_rows), :] = rows_q.astype(jnp.bfloat16)
+                return z
+
+            lax.fori_loop(0, n, pack, 0)
+
+        def attach_sums():
             def one(q, z):
                 first = q * cols
                 lo = pl.multiple_of(first // LANES * LANES, LANES)
                 s = lax.rem(first, LANES)
-                sides = []
-                for t, shift in ((0, lax.rem(LANES - s, LANES)), (1, lax.rem(LANES + half_lane - s, LANES))):
-                    a = pltpu.roll(sums[h, t, :, pl.ds(lo, LANES)], shift, axis=1)
-                    b = pltpu.roll(sums[h, t, :, pl.ds(lo + LANES, LANES)], shift, axis=1)
-                    sides.append(jnp.where(lane - t * half_lane + s < LANES, a, b))
-                msg[h, q] = jnp.where(left, sides[0], sides[1])
+                for h in range(2):
+                    sides = []
+                    for t, shift in ((0, lax.rem(LANES - s, LANES)), (1, lax.rem(LANES + half_lane - s, LANES))):
+                        a = pltpu.roll(sums[h, t, :, pl.ds(lo, LANES)], shift, axis=1)
+                        b = pltpu.roll(sums[h, t, :, pl.ds(lo + LANES, LANES)], shift, axis=1)
+                        sides.append(jnp.where(lane - t * half_lane + s < LANES, a, b))
+                    p = jnp.where(left, sides[0], sides[1])
+                    high = p.astype(jnp.bfloat16).astype(jnp.float32)
+                    parts = jnp.concatenate([high, p - high], axis=0).astype(jnp.bfloat16)
+                    code_b[q, pl.ds(cols * few + h * tile, tile), :] = parts
                 return z
 
             lax.fori_loop(0, n, one, 0)
-            inbox[h, me] = msg[h, me]
+
+        def partial(h, s):
+            parts = got_b[s, pl.ds(cols * few + h * tile, tile), :].astype(jnp.float32)
+            return parts[:SUBS] + parts[SUBS:]
 
         def piece_to(m, q):
             a, first, size = pieces[m]
-            whole = cols * stretches[a][1]
-            return pltpu.make_async_remote_copy(
-                codes[a].at[pl.ds(pl.multiple_of(q * whole + first, 16), size)], gots[a].at[me, pl.ds(first, size)],
+            at = pl.ds(first, size)
+            return pltpu.make_async_remote_copy(
+                codes[a].at[q, at], gots[a].at[me, at],
                 send_sem.at[m], recv_sem.at[m, me], device_id={"shard": q}, device_id_type=MESH,
             )
 
@@ -132,27 +153,13 @@
 
         def all_pieces(m):
             a, _, size = pieces[m]
-            ref = codes[a].at[pl.ds(0, (n - 1) * size)]
+            ref = codes[a].at[pl.ds(0, n - 1), pl.ds(0, size)]
             return pltpu.make_async_remote_copy(
                 ref, ref, send_sem.at[m], recv_sem.at[m, 0], device_id={"shard": me}, device_id_type=MESH
             )
 
-        def sums_to(h, q):
-            return pltpu.make_async_remote_copy(
-                msg.at[h, q], inbox.at[h, me], sums_send.at[h], sums_recv.at[h], device_id={"shard": q}, device_id_type=MESH
-            )
-
-        def all_sums(h):
-            src, dst = msg.at[h, pl.ds(0, n - 1)], inbox.at[h, pl.ds(0, n - 1)]
-            return pltpu.make_async_remote_copy(
-                src, dst, sums_send.at[h], sums_recv.at[h], device_id={"shard": me}, device_id_type=MESH
-            )
-
         def own(a):
-            size = cols * stretches[a][1]
-            return pltpu.make_async_copy(
-                codes[a].at[pl.ds(pl.multiple_of(me * size, 16), size)], gots[a].at[me], own_sem.at[a]
-            )
+            return pltpu.make_async_copy(codes[a].at[me], gots[a].at[me], own_sem.at[a])
 
         def tile_to(q):
             return pltpu.make_async_remote_copy(
@@ -168,6 +175,10 @@
                 rin.at[k], rin.at[k], pair_sem.at[0], pair_sem.at[1],
                 device_id={"shard": my_chip * 2 + 1 - my_k}, device_id_type=MESH,
             )
+
+        def send(m):
+            for q in peers:
+                piece_to(m, q).start()
 
         for a in range(3):
             for t in range(2):
@@ -180,19 +191,15 @@
                 rtile[...] = jnp.concatenate([folded[:SUBS], folded[SUBS:]], axis=1).astype(jnp.bfloat16)
                 rin[my_k, my_chip] = rtile[...]
                 pl.semaphore_wait(barrier, n - 1 + n_z - 1)
-            else:
-                message(a - 1)
-                for q in peers:
-                    sums_to(a - 1, q).start()
-            for m in range(len(pieces)):
-                if pieces[m][0] == a:
-                    for q in peers:
-                        piece_to(m, q).start()
-            own(a).start()
-            if a == 0:
+                send(0)
                 for d, q in zip(order, peers):
                     if d % 2 == 0:
                         tile_to(q).start()
+        attach_sums()
+        for m in range(1, len(pieces)):
+            send(m)
+        for a in range(3):
+            own(a).start()
 
         all_tiles().wait_recv()
         to_partner(my_k).start()
@@ -218,8 +225,7 @@
         orr[pl.ds(pl.multiple_of(plane * experts, experts), experts), :] = zbuf[...]
 
         def factors(h):
-            all_sums(h).wait_recv()
-            total = lax.fori_loop(0, n, lambda s, t: t + inbox[h, s], jnp.zeros((SUBS, LANES), jnp.float32))
+            total = lax.fori_loop(0, n, lambda s, t: t + partial(h, s), jnp.zeros((SUBS, LANES), jnp.float32))
             scale = jnp.sqrt(total)
             osg[pl.ds(h * SUBS, SUBS), :] = scale[:, :cols]
             osu[pl.ds(h * SUBS, SUBS), :] = across_lanes(scale)[:, :cols]
@@ -227,8 +233,8 @@
             some = jnp.logical_and(used, total > 0)
 
             def one(c, z):
-                a = jnp.where(some, jnp.sqrt(inbox[h, 2 * c]) * each, 0.0)
-                b = jnp.where(some, jnp.sqrt(inbox[h, 2 * c + 1]) * each, 0.0)
+                a = jnp.where(some, jnp.sqrt(partial(h, 2 * c)) * each, 0.0)
+                b = jnp.where(some, jnp.sqrt(partial(h, 2 * c + 1)) * each, 0.0)
                 turned = across_lanes(jnp.where(left, b, a))
                 for t, f in ((0, jnp.where(left, a, turned)), (1, jnp.where(left, turned, b))):
                     at = pl.ds(pl.multiple_of(t * chips * SUBS + c * SUBS, SUBS), SUBS)
@@ -246,8 +252,8 @@
             def two(p, z):
                 pick = jnp.where(source == 2 * p, 1.0, 0.0).astype(jnp.bfloat16)
                 wide = jnp.dot(lhs, pick, preferred_element_type=jnp.float32)
-                spread[2 * p] = wide[:, :LANES]
-                spread[2 * p + 1] = wide[:, LANES:]
+                spread[h, 2 * p] = wide[:, :LANES]
+                spread[h, 2 * p + 1] = wide[:, LANES:]
                 return z
 
             lax.fori_loop(0, cols // 2, two, 0)
@@ -261,8 +267,8 @@
             turned = across_lanes(jnp.where(left2, two, one))
             return jnp.where(left2, one, turned), jnp.where(left2, turned, two)
 
-        def decode(ms, first, count):
-            h = 0 if pieces[ms[0]][0] < 2 else 1
+        def decode(m, first, count):
+            h = pieces[m][0] // 2
 
             def chip(i, z):
                 dc = lax.rem(START // 2 + MIX * i, chips)
@@ -272,13 +278,12 @@
                 for k in range(2):
                     @pl.when(2 * at + k != me)
                     def arrival():
-                        for m in ms:
-                            piece_from(m, 2 * at + k).wait_recv()
+                        piece_from(m, 2 * at + k).wait_recv()
 
                 lanes_out = pl.ds(pl.multiple_of(at * LANES, LANES), LANES)
 
                 def put(t, j, x):
-                    f = spread[j, pl.ds(pl.multiple_of(t * chips * SUBS + at * SUBS, SUBS), SUBS), :]
+                    f = spread[h, j, pl.ds(pl.multiple_of(t * chips * SUBS + at * SUBS, SUBS), SUBS), :]
                     (og, ou)[t][j, pl.ds(h * SUBS, SUBS), lanes_out] = (x * f).astype(jnp.bfloat16)
 
                 if h:
@@ -302,15 +307,13 @@
 
             lax.fori_loop(0, chips, chip, 0)
 
+        for a in range(3):
+            own(a).wait()
+        for q in peers:
+            piece_from(1, q).wait_recv()
         factors(0)
-        own(0).wait()
-        own(1).wait()
-        decode((0, 1), 0, cols)
+        decode(0, 0, cols)
         factors(1)
-        own(2).wait()
-        for i in range(len(PARTS)):
-            decode((2 + i,), sum(PARTS[:i]), PARTS[i])
-
         for d in range(1, n_z):
             z = lax.rem(plane + d, n_z)
             across(d, plane).wait_send()
@@ -318,8 +321,8 @@
             orr[pl.ds(pl.multiple_of(z * experts, experts), experts), :] = zgot[z]
         to_partner(my_k).wait_send()
         all_tiles().wait_send()
-        for h in range(2):
-            all_sums(h).wait_send()
+        for i in range(len(PARTS)):
+            decode(2 + i, sum(PARTS[:i]), PARTS[i])
         for m in range(len(pieces)):
             all_pieces(m).wait_send()
 
@@ -369,29 +372,22 @@
             scratch_shapes=[
                 pltpu.VMEM((experts, rows, width), f32),
                 pltpu.VMEM((experts, rows, width), f32),
-                pltpu.VMEM((LANES * SUBS, LANES), f32),
-                pltpu.VMEM((width * few, LANES), bf16),
-                pltpu.VMEM((width * few, LANES), bf16),
-                pltpu.VMEM((width * SUBS, LANES), bf16),
-                pltpu.VMEM((n, cols * few, LANES), bf16),
-                pltpu.VMEM((n, cols * few, LANES), bf16),
-                pltpu.VMEM((n, cols * SUBS, LANES), bf16),
+                pltpu.VMEM((width * SUBS, LANES), f32),
+                *[pltpu.VMEM((n, r, LANES), bf16) for r in (cols * few, cols * few + 4 * SUBS, cols * SUBS)] * 2,
                 pltpu.VMEM((2, 2, SUBS, width + LANES), f32),
-                pltpu.VMEM((2, n, SUBS, LANES), f32),
-                pltpu.VMEM((2, n, SUBS, LANES), f32),
                 pltpu.VMEM((n * SUBS, 2 * LANES), f32),
-                pltpu.VMEM((cols, n * SUBS, LANES), f32),
+                pltpu.VMEM((2, cols, n * SUBS, LANES), f32),
                 pltpu.VMEM((experts, rows), f32),
                 pltpu.VMEM((1, rows), f32),
                 pltpu.VMEM((SUBS, LANES), bf16),
                 pltpu.VMEM((2, n // 2, SUBS, LANES), bf16),
                 pltpu.VMEM((experts, depth), bf16),
                 pltpu.VMEM((n_z, experts, depth), bf16),
-                dma((3, 2)), dma((2,)), dma((3,)), dma((sent,)), dma((sent, n)), dma((2,)), dma((2,)),
+                dma((3, 2)), dma((2,)), dma((3,)), dma((sent,)), dma((sent, n)),
                 dma, dma, dma((2,)), dma((n_z,)), dma((n_z,)),
             ],
             compiler_params=pltpu.CompilerParams(
-                collective_id=0, has_side_effects=True, vmem_limit_bytes=48 * 2**20
+                collective_id=0, has_side_effects=True, vmem_limit_bytes=45 * 2**20
             ),
         )(master_gate, master_up, in_hbm(router_weight.T), in_hbm(router_gain[None, :]))
         og, ou, osg, osu, orr = pl.pallas_call(

time: 82.1 us -> 81.8 us (level)
  no operation moved by 1% of the time
where the time goes in v4:
time: 81.8 us; the launch traced here: 81.6 us
  Pallas kernels  81 us (99%)
    pallas_call x1, Pallas kernels, local(): pl.pallas_call(make_kernel(experts, rows, width, cols, n_y, n_x, n_z), ou...  78.3 us
    pallas_call x1, Pallas kernels, local(): pl.pallas_call(put_out, out_shape=shapes, in_specs=[pl.BlockSpec(memory_s...  2.66 us

profile of v4, /device:TPU:1, one launch (start us, length us, event | category | flops | bytes accessed | tf_op | source)
XLA Modules:
  0.0 81.6 jit_solution(6907436960290503958)
XLA Ops:
  0.6 78.3 %shard_map.83 = (bf16[44,16,2048]{2,1,0:T(8,128)(2,1)S(1)}, bf16[44,16,2048]{2,1,0:T(8,128)(2,1)S(1)}, f32[16,44]{1,0:T(8,128)S(1)}, f32[16,44]{1,0:T(8,128)S(1)}, bf16[64,2048]{1,0:T(8,128)(2,1)S(1)}) custom-call(f32[16,64,1408]{2,1,0:T(8,128)} %gate.1, f32[16,64,1408]{2,1,0:T(8,128)} %up.1, f32[16,64]{1,0:T(8,128)} %bitcast.5, f32[1,64]{1,0:T(1,128)} %bitcast.6), custom_call_target="tpu_custom_call" | custom-call | tf_op jit(solution)/shard_map/pallas_call | solution.py:367
  79.0 2.7 %shard_map.84 = (bf16[44,16,2048]{2,1,0:T(8,128)(2,1)}, bf16[44,16,2048]{2,1,0:T(8,128)(2,1)}, f32[16,44]{1,0:T(8,128)}, f32[16,44]{1,0:T(8,128)}, bf16[64,2048]{1,0:T(8,128)(2,1)}) custom-call(bf16[44,16,2048]{2,1,0:T(8,128)(2,1)S(1)} %get-tuple-element.15.refs_0_, bf16[44,16,2048]{2,1,0:T(8,128)(2,1)S(1)} %get-tuple-element.16.refs_1_, ...), custom_call_target="tpu_custom_call" | custom-call | tf_op jit(solution)/shard_map/pallas_call | solution.py:393

commit v5 on v4

--- a/solution.py
+++ b/solution.py
@@ -10,7 +10,7 @@
 SUBS = 8
 SPAN = 250.0
 FLOOR = 124.0
-MIX, START = 11, 16
+MIX, START = 23, 16
 PARTS = (24, 20)
 
 
@@ -33,8 +33,8 @@
 
     def kernel(gate, up, router, gain, og, ou, osg, osu, orr,
                xg, xu, stage, code_a, code_b, code_c, got_a, got_b, got_c, sums, share, spread,
-               xr, xgain, rtile, rin, zbuf, zgot,
-               in_sem, small_sem, own_sem, send_sem, recv_sem, rsend, rrecv, pair_sem, zsend, zrecv):
+               xr, xgain, zbuf, zgot,
+               in_sem, small_sem, own_sem, send_sem, recv_sem, zsend, zrecv):
         codes, gots = (code_a, code_b, code_c), (got_a, got_b, got_c)
         me = lax.axis_index("shard")
         plane = lax.axis_index("expert")
@@ -80,7 +80,9 @@
         left = lane < half_lane
         left2 = lax.broadcasted_iota(jnp.int32, (2 * SUBS, LANES), 1) < half_lane
         upper = row < few
-        used = lax.rem(lane, half_lane) < cols
+        lane2 = lax.broadcasted_iota(jnp.int32, (2 * SUBS, LANES), 1)
+        used, used2 = lax.rem(lane, half_lane) < cols, lax.rem(lane2, half_lane) < cols
+        quarter = half_lane // 4
 
         def across_lanes(v):
             return pltpu.roll(v, half_lane, axis=1)
@@ -114,6 +116,15 @@
             lax.fori_loop(0, n, pack, 0)
 
         def attach_sums():
+            for c in small:
+                c.wait()
+            folded = xr[...] * xgain[...]
+            folded = jnp.concatenate([folded, folded], axis=1)
+            riders = []
+            for h in range(2):
+                near, far = (pltpu.roll(folded, at - i * quarter, axis=1) for at, i in ((cols, 2 * h), (half_lane + cols, 2 * h + 1)))
+                riders.append(jnp.where(left2, near, far))
+
             def one(q, z):
                 first = q * cols
                 lo = pl.multiple_of(first // LANES * LANES, LANES)
@@ -126,8 +137,8 @@
                         sides.append(jnp.where(lane - t * half_lane + s < LANES, a, b))
                     p = jnp.where(left, sides[0], sides[1])
                     high = p.astype(jnp.bfloat16).astype(jnp.float32)
-                    parts = jnp.concatenate([high, p - high], axis=0).astype(jnp.bfloat16)
-                    code_b[q, pl.ds(cols * few + h * tile, tile), :] = parts
+                    parts = jnp.where(used2, jnp.concatenate([high, p - high], axis=0), riders[h])
+                    code_b[q, pl.ds(cols * few + h * tile, tile), :] = parts.astype(jnp.bfloat16)
                 return z
 
             lax.fori_loop(0, n, one, 0)
@@ -161,21 +172,6 @@
         def own(a):
             return pltpu.make_async_copy(codes[a].at[me], gots[a].at[me], own_sem.at[a])
 
-        def tile_to(q):
-            return pltpu.make_async_remote_copy(
-                rtile, rin.at[my_k, my_chip], rsend, rrecv, device_id={"shard": q}, device_id_type=MESH
-            )
-
-        def all_tiles():
-            ref = rin.at[0, pl.ds(0, chips - 1)]
-            return pltpu.make_async_remote_copy(ref, ref, rsend, rrecv, device_id={"shard": me}, device_id_type=MESH)
-
-        def to_partner(k):
-            return pltpu.make_async_remote_copy(
-                rin.at[k], rin.at[k], pair_sem.at[0], pair_sem.at[1],
-                device_id={"shard": my_chip * 2 + 1 - my_k}, device_id_type=MESH,
-            )
-
         def send(m):
             for q in peers:
                 piece_to(m, q).start()
@@ -185,31 +181,29 @@
                 load(a, t).wait()
             produce(a)
             if a == 0:
-                for c in small:
-                    c.wait()
-                folded = xr[...] * xgain[...]
-                rtile[...] = jnp.concatenate([folded[:SUBS], folded[SUBS:]], axis=1).astype(jnp.bfloat16)
-                rin[my_k, my_chip] = rtile[...]
                 pl.semaphore_wait(barrier, n - 1 + n_z - 1)
                 send(0)
-                for d, q in zip(order, peers):
-                    if d % 2 == 0:
-                        tile_to(q).start()
         attach_sums()
         for m in range(1, len(pieces)):
             send(m)
         for a in range(3):
             own(a).start()
 
-        all_tiles().wait_recv()
-        to_partner(my_k).start()
-        to_partner(1 - my_k).wait_recv()
+        for a in range(3):
+            own(a).wait()
+        for q in peers:
+            piece_from(1, q).wait_recv()
 
         def join(c, z):
-            a, b = rin[0, c].astype(jnp.float32), rin[1, c].astype(jnp.float32)
-            low = jnp.where(left, a, across_lanes(b))
-            high = jnp.where(left, across_lanes(a), b)
-            zbuf[:, pl.ds(pl.multiple_of(c * LANES, LANES), LANES)] = jnp.concatenate([low, high], axis=0).astype(jnp.bfloat16)
+            whole = jnp.zeros((2 * SUBS, LANES), jnp.float32)
+            for k in range(2):
+                for h in range(2):
+                    v = got_b[2 * c + k, pl.ds(cols * few + h * tile, tile), :].astype(jnp.float32)
+                    for side in range(2):
+                        to = k * half_lane + (2 * h + side) * quarter
+                        moved = pltpu.roll(v, (to - side * half_lane - cols) % LANES, axis=1)
+                        whole = jnp.where(jnp.logical_and(lane2 >= to, lane2 < to + quarter), moved, whole)
+            zbuf[:, pl.ds(pl.multiple_of(c * LANES, LANES), LANES)] = whole.astype(jnp.bfloat16)
             return z
 
         lax.fori_loop(0, chips, join, 0)
@@ -307,10 +301,6 @@
 
             lax.fori_loop(0, chips, chip, 0)
 
-        for a in range(3):
-            own(a).wait()
-        for q in peers:
-            piece_from(1, q).wait_recv()
         factors(0)
         decode(0, 0, cols)
         factors(1)
@@ -319,8 +309,6 @@
             across(d, plane).wait_send()
             across(d, z).wait_recv()
             orr[pl.ds(pl.multiple_of(z * experts, experts), experts), :] = zgot[z]
-        to_partner(my_k).wait_send()
-        all_tiles().wait_send()
         for i in range(len(PARTS)):
             decode(2 + i, sum(PARTS[:i]), PARTS[i])
         for m in range(len(pieces)):
@@ -372,19 +360,17 @@
             scratch_shapes=[
                 pltpu.VMEM((experts, rows, width), f32),
                 pltpu.VMEM((experts, rows, width), f32),
-                pltpu.VMEM((width * SUBS, LANES), f32),
+                pltpu.VMEM((width * SUBS + SUBS, LANES), f32),
                 *[pltpu.VMEM((n, r, LANES), bf16) for r in (cols * few, cols * few + 4 * SUBS, cols * SUBS)] * 2,
                 pltpu.VMEM((2, 2, SUBS, width + LANES), f32),
                 pltpu.VMEM((n * SUBS, 2 * LANES), f32),
                 pltpu.VMEM((2, cols, n * SUBS, LANES), f32),
                 pltpu.VMEM((experts, rows), f32),
                 pltpu.VMEM((1, rows), f32),
-                pltpu.VMEM((SUBS, LANES), bf16),
-                pltpu.VMEM((2, n // 2, SUBS, LANES), bf16),
                 pltpu.VMEM((experts, depth), bf16),
                 pltpu.VMEM((n_z, experts, depth), bf16),
                 dma((3, 2)), dma((2,)), dma((3,)), dma((sent,)), dma((sent, n)),
-                dma, dma, dma((2,)), dma((n_z,)), dma((n_z,)),
+                dma((n_z,)), dma((n_z,)),
             ],
             compiler_params=pltpu.CompilerParams(
                 collective_id=0, has_side_effects=True, vmem_limit_bytes=45 * 2**20

time: 81.8 us -> 80.6 us (0.985)
  Pallas kernels: 81 us -> 79.9 us
    pallas_call x1, Pallas kernels: 78.3 us -> 77.2 us  [local(): pl.pallas_call(make_kernel(experts, rows, width, cols, n_y, n_x, n_z), ou...]
where the time goes in v5:
time: 80.6 us; the launch traced here: 80.5 us
  Pallas kernels  79.9 us (99%)
    pallas_call x1, Pallas kernels, local(): pl.pallas_call(make_kernel(experts, rows, width, cols, n_y, n_x, n_z), ou...  77.2 us
    pallas_call x1, Pallas kernels, local(): pl.pallas_call(put_out, out_shape=shapes, in_specs=[pl.BlockSpec(memory_s...  2.66 us

profile of v5, /device:TPU:1, one launch (start us, length us, event | category | flops | bytes accessed | tf_op | source)
XLA Modules:
  0.0 80.5 jit_solution(13584303598954988962)
XLA Ops:
  0.6 77.2 %shard_map.83 = (bf16[44,16,2048]{2,1,0:T(8,128)(2,1)S(1)}, bf16[44,16,2048]{2,1,0:T(8,128)(2,1)S(1)}, f32[16,44]{1,0:T(8,128)S(1)}, f32[16,44]{1,0:T(8,128)S(1)}, bf16[64,2048]{1,0:T(8,128)(2,1)S(1)}) custom-call(f32[16,64,1408]{2,1,0:T(8,128)} %gate.1, f32[16,64,1408]{2,1,0:T(8,128)} %up.1, f32[16,64]{1,0:T(8,128)} %bitcast.5, f32[1,64]{1,0:T(1,128)} %bitcast.6), custom_call_target="tpu_custom_call" | custom-call | tf_op jit(solution)/shard_map/pallas_call | solution.py:355
  77.8 2.7 %shard_map.84 = (bf16[44,16,2048]{2,1,0:T(8,128)(2,1)}, bf16[44,16,2048]{2,1,0:T(8,128)(2,1)}, f32[16,44]{1,0:T(8,128)}, f32[16,44]{1,0:T(8,128)}, bf16[64,2048]{1,0:T(8,128)(2,1)}) custom-call(bf16[44,16,2048]{2,1,0:T(8,128)(2,1)S(1)} %get-tuple-element.15.refs_0_, bf16[44,16,2048]{2,1,0:T(8,128)(2,1)S(1)} %get-tuple-element.16.refs_1_, ...), custom_call_target="tpu_custom_call" | custom-call | tf_op jit(solution)/shard_map/pallas_call | solution.py:379

commit v6 on v5

--- a/solution.py
+++ b/solution.py
@@ -10,7 +10,7 @@
 SUBS = 8
 SPAN = 250.0
 FLOOR = 124.0
-MIX, START = 23, 16
+MIX, START = 23, 8
 PARTS = (24, 20)
 
 

time: 80.6 us -> 79.8 us (0.990)
  no operation moved by 1% of the time
where the time goes in v6:
time: 79.8 us; the launch traced here: 79.7 us
  Pallas kernels  79.1 us (99%)
    pallas_call x1, Pallas kernels, local(): pl.pallas_call(make_kernel(experts, rows, width, cols, n_y, n_x, n_z), ou...  76.4 us
    pallas_call x1, Pallas kernels, local(): pl.pallas_call(put_out, out_shape=shapes, in_specs=[pl.BlockSpec(memory_s...  2.66 us

profile of v6, /device:TPU:1, one launch (start us, length us, event | category | flops | bytes accessed | tf_op | source)
XLA Modules:
  0.0 79.7 jit_solution(127532775662567637)
XLA Ops:
  0.6 76.4 %shard_map.83 = (bf16[44,16,2048]{2,1,0:T(8,128)(2,1)S(1)}, bf16[44,16,2048]{2,1,0:T(8,128)(2,1)S(1)}, f32[16,44]{1,0:T(8,128)S(1)}, f32[16,44]{1,0:T(8,128)S(1)}, bf16[64,2048]{1,0:T(8,128)(2,1)S(1)}) custom-call(f32[16,64,1408]{2,1,0:T(8,128)} %gate.1, f32[16,64,1408]{2,1,0:T(8,128)} %up.1, f32[16,64]{1,0:T(8,128)} %bitcast.5, f32[1,64]{1,0:T(1,128)} %bitcast.6), custom_call_target="tpu_custom_call" | custom-call | tf_op jit(solution)/shard_map/pallas_call | solution.py:355
  77.0 2.7 %shard_map.84 = (bf16[44,16,2048]{2,1,0:T(8,128)(2,1)}, bf16[44,16,2048]{2,1,0:T(8,128)(2,1)}, f32[16,44]{1,0:T(8,128)}, f32[16,44]{1,0:T(8,128)}, bf16[64,2048]{1,0:T(8,128)(2,1)}) custom-call(bf16[44,16,2048]{2,1,0:T(8,128)(2,1)S(1)} %get-tuple-element.15.refs_0_, bf16[44,16,2048]{2,1,0:T(8,128)(2,1)S(1)} %get-tuple-element.16.refs_1_, ...), custom_call_target="tpu_custom_call" | custom-call | tf_op jit(solution)/shard_map/pallas_call | solution.py:379

commit v7 on v6

--- a/solution.py
+++ b/solution.py
@@ -11,7 +11,7 @@
 SPAN = 250.0
 FLOOR = 124.0
 MIX, START = 23, 8
-PARTS = (24, 20)
+PARTS = (22, 22)
 
 
 def encoded(x, partial):

time: 79.8 us -> 79.6 us (level)
  no operation moved by 1% of the time
where the time goes in v7:
time: 79.6 us; the launch traced here: 79.5 us
  Pallas kernels  78.8 us (99%)
    pallas_call x1, Pallas kernels, local(): pl.pallas_call(make_kernel(experts, rows, width, cols, n_y, n_x, n_z), ou...  76.2 us
    pallas_call x1, Pallas kernels, local(): pl.pallas_call(put_out, out_shape=shapes, in_specs=[pl.BlockSpec(memory_s...  2.66 us

profile of v7, /device:TPU:1, one launch (start us, length us, event | category | flops | bytes accessed | tf_op | source)
XLA Modules:
  0.0 79.5 jit_solution(13795506037620066119)
XLA Ops:
  0.6 76.2 %shard_map.83 = (bf16[44,16,2048]{2,1,0:T(8,128)(2,1)S(1)}, bf16[44,16,2048]{2,1,0:T(8,128)(2,1)S(1)}, f32[16,44]{1,0:T(8,128)S(1)}, f32[16,44]{1,0:T(8,128)S(1)}, bf16[64,2048]{1,0:T(8,128)(2,1)S(1)}) custom-call(f32[16,64,1408]{2,1,0:T(8,128)} %gate.1, f32[16,64,1408]{2,1,0:T(8,128)} %up.1, f32[16,64]{1,0:T(8,128)} %bitcast.5, f32[1,64]{1,0:T(1,128)} %bitcast.6), custom_call_target="tpu_custom_call" | custom-call | tf_op jit(solution)/shard_map/pallas_call | solution.py:355
  76.8 2.7 %shard_map.84 = (bf16[44,16,2048]{2,1,0:T(8,128)(2,1)}, bf16[44,16,2048]{2,1,0:T(8,128)(2,1)}, f32[16,44]{1,0:T(8,128)}, f32[16,44]{1,0:T(8,128)}, bf16[64,2048]{1,0:T(8,128)(2,1)}) custom-call(bf16[44,16,2048]{2,1,0:T(8,128)(2,1)S(1)} %get-tuple-element.15.refs_0_, bf16[44,16,2048]{2,1,0:T(8,128)(2,1)S(1)} %get-tuple-element.16.refs_1_, ...), custom_call_target="tpu_custom_call" | custom-call | tf_op jit(solution)/shard_map/pallas_call | solution.py:379
